TPU v7x, 256 devices: a whole 4x4x8 slice. The times are simulated.
256 devices in a mesh: gx: 16 (over z, x_lo), gz: 16 (over y, x_hi, core).
Axes of the slice: x: 4 (x_hi: 2, x_lo: 2; x = x_hi * 2 + x_lo), y: 4, z: 8, core: 2. Of those that a mesh axis runs over, the one named last changes fastest.
Arguments:
- velocity: float32 [3, 128, 512, 384], P(None, 'gx', 'gz'), may hold values from -6 to 6
- y_gap: float32 [385], replicated, may hold values from 0.2 to 2
Outputs:
- eddy_visc: float32 [128, 512, 384], P('gx', 'gz')
- lm_field: float32 [128, 512, 384], P('gx', 'gz')
- mm_field: float32 [128, 512, 384], P('gx', 'gz')
- coefficient: float32 [384], replicated
All inputs are finite; a program needn't handle non-finite values.
Results may differ from a plain program's by a relative error of at most 0.00002.
Values sent between devices are 32-bit elements; how exact they have to be, the bound alone decides.
A program may use at most 64 MiB of HBM per device.

v0:
```python
import functools

import jax
import jax.numpy as jnp
from jax import lax
from jax.sharding import Mesh
from jax.sharding import PartitionSpec as P

GX_GZ = ("gx_0", "gx_1", "gz_0", "gz_1", "gz_2")
GX = ("gx_0", "gx_1")
GZ = ("gz_0", "gz_1", "gz_2")


WEIGHTS = (1.0, 1.0, 1.0, 2.0, 2.0, 2.0)


def extended(array, sides, width):
    for axis, dim in sides:
        size, length = (lax.axis_size(axis), array.shape[dim])
        up = [(i, (i + 1) % size) for i in range(size)]
        down = [(j, i) for i, j in up]
        last = lax.slice_in_dim(array, length - width, length, axis=dim)
        leading = lax.slice_in_dim(array, 0, width, axis=dim)
        before = lax.ppermute(last, axis, up)
        after = lax.ppermute(leading, axis, down)
        array = jnp.concatenate([before, array, after], axis=dim)
    return array


def over_axes(array, axes):
    return functools.reduce(lax.psum, axes, array)


def wall_slope(values, y_gap):
    padded = jnp.pad(values, [(0, 0)] * (values.ndim - 1) + [(1, 1)])
    return (padded[..., 2:] - padded[..., :-2]) / (y_gap[:-1] + y_gap[1:])


def strain_parts(slope_x, slope_y, slope_z):
    return jnp.stack(
        [
            slope_x[0],
            slope_y[1],
            slope_z[2],
            0.5 * (slope_y[0] + slope_x[1]),
            0.5 * (slope_z[0] + slope_x[2]),
            0.5 * (slope_z[1] + slope_y[2]),
        ]
    )


def contract(first_part, second_part):
    summed = first_part[0] * second_part[0]
    for component in range(1, 6):
        summed = summed + WEIGHTS[component] * first_part[component] * second_part[component]
    return summed


def magnitude(strain):
    return jnp.sqrt(2.0 * contract(strain, strain))


def pair_products(speeds):
    return jnp.stack(
        [
            speeds[0] * speeds[0],
            speeds[1] * speeds[1],
            speeds[2] * speeds[2],
            speeds[0] * speeds[1],
            speeds[0] * speeds[2],
            speeds[1] * speeds[2],
        ]
    )


def width_square(y_gap):
    return (0.5 * (y_gap[:-1] + y_gap[1:])) ** (2.0 / 3.0)


def germano(smooth_velocity, smooth_pairs, smooth_stress, test_strain, width_sq):
    leonard = smooth_pairs - pair_products(smooth_velocity)
    model_term = 2.0 * width_sq * (smooth_stress - 4.0 * magnitude(test_strain) * test_strain)
    return (contract(leonard, model_term), contract(model_term, model_term))


def rim_strain(padded, y_gap):
    slope_x = (padded[:, 2:, 1:-1] - padded[:, :-2, 1:-1]) * 0.5
    slope_z = (padded[:, 1:-1, 2:] - padded[:, 1:-1, :-2]) * 0.5
    slope_y = wall_slope(padded[:, 1:-1, 1:-1], y_gap)
    return strain_parts(slope_x, slope_y, slope_z)


def rim_filter(values):
    along_x = 0.25 * values[:, :-2] + 0.5 * values[:, 1:-1] + 0.25 * values[:, 2:]
    return 0.25 * along_x[:, :, :-2] + 0.5 * along_x[:, :, 1:-1] + 0.25 * along_x[:, :, 2:]


def per_device(velocity, y_gap):
    width_sq = width_square(y_gap)
    padded = extended(velocity, ((GX, 1), (GZ, 2)), 2)
    strain_wide = rim_strain(padded, y_gap)
    size_wide = magnitude(strain_wide)
    inner = padded[:, 1:-1, 1:-1]
    smooth_pairs = rim_filter(pair_products(inner))
    smooth_stress = rim_filter(size_wide * strain_wide)
    smooth_wide = rim_filter(padded)
    smooth_velocity = smooth_wide[:, 1:-1, 1:-1]
    test_strain = rim_strain(smooth_wide, y_gap)
    strain_size = size_wide[1:-1, 1:-1]
    lm_field, mm_field = germano(
        smooth_velocity, smooth_pairs, smooth_stress, test_strain, width_sq
    )
    planes = velocity.shape[1] * lax.axis_size(GX) * velocity.shape[2] * lax.axis_size(GZ)
    plane_pair = jnp.stack([jnp.sum(lm_field, axis=(0, 1)), jnp.sum(mm_field, axis=(0, 1))])
    total_pair = over_axes(plane_pair, GX_GZ)
    coefficient = total_pair[0] / planes / (total_pair[1] / planes + 1e-06)
    eddy_visc = coefficient * width_sq * strain_size
    return (eddy_visc, lm_field, mm_field, coefficient)


def solution(mesh):
    torus = Mesh(mesh.devices.reshape(8, 2, 4, 2, 2), ("gx_0", "gx_1", "gz_0", "gz_1", "gz_2"))
    return jax.shard_map(
        per_device,
        mesh=torus,
        in_specs=(P(None, GX, GZ, None), P()),
        out_specs=(P(GX, GZ, None), P(GX, GZ, None), P(GX, GZ, None), P()),
        check_vma=False,
    )
```

profile of v0, /device:TPU:1, one launch (start us, length us, event | category | flops | bytes accessed | tf_op | source)
XLA Modules:
  0.0 85.4 jit_solution(11277026666586406063)
XLA Ops:
  0.6 0.0 copy-start
  0.6 0.0 copy-start.2
  0.7 1.2 %fusion.70 = (f32[3,2,32,384]{3,2,1,0:T(8,128)S(1)}, f32[3,2,32,384]{3,2,1,0:T(8,128)S(1)}) fusion(f32[3,8,32,384]{3,2,1,0:T(8,128)} %param.2), kind=kLoop, calls=%fused_computation.159 | loop fusion | bytes 1179648 | tf_op jit(solution)/shard_map/slice | solution.py:23
  1.8 2.1 %collective-permute-start = (f32[3,2,32,384]{3,2,1,0:T(8,128)S(1)}, f32[3,2,32,384]{3,2,1,0:T(8,128)S(1)}, u32[]{:S(2)}, u32[]{:S(2)}) collective-permute-start(f32[3,2,32,384]{3,2,1,0:T(8,128)S(1)} %get-tuple-element.30), channel_id=1, source_target_pairs={{0,16},{16,32},{32,48},{48,64},{64,80},{80,96},{96,112},{112,128},... | collective-permute-start | bytes 884744 | tf_op jit(solution)/shard_map/ppermute | solution.py:24
  3.9 5.4 %collective-permute-start.1 = (f32[3,2,32,384]{3,2,1,0:T(8,128)S(1)}, f32[3,2,32,384]{3,2,1,0:T(8,128)S(1)}, u32[]{:S(2)}, u32[]{:S(2)}) collective-permute-start(f32[3,2,32,384]{3,2,1,0:T(8,128)S(1)} %get-tuple-element.29), channel_id=1, source_target_pairs={{16,0},{32,16},{48,32},{64,48},{80,64},{96,80},{112,96},{128,112},... | collective-permute-start | bytes 884744 | tf_op jit(solution)/shard_map/ppermute | solution.py:25
  9.3 6.7 %collective-permute-done = f32[3,2,32,384]{3,2,1,0:T(8,128)S(1)} collective-permute-done((f32[3,2,32,384]{3,2,1,0:T(8,128)S(1)}, f32[3,2,32,384]{3,2,1,0:T(8,128)S(1)}, u32[]{:S(2)}, u32[]{:S(2)}) %collective-permute-start) | collective-permute-done | bytes 294944 | tf_op jit(solution)/shard_map/ppermute | solution.py:24
  16.0 0.1 constant_dynamic-update-slice_fusion.1
  16.1 1.7 %collective-permute-done.1 = f32[3,2,32,384]{3,2,1,0:T(8,128)S(1)} collective-permute-done((f32[3,2,32,384]{3,2,1,0:T(8,128)S(1)}, f32[3,2,32,384]{3,2,1,0:T(8,128)S(1)}, u32[]{:S(2)}, u32[]{:S(2)}) %collective-permute-start.1) | collective-permute-done | bytes 294944 | tf_op jit(solution)/shard_map/ppermute | solution.py:25
  17.9 0.1 fusion.69
  18.0 2.1 %collective-permute-start.3 = (f32[3,12,2,384]{3,2,1,0:T(2,128)S(1)}, f32[3,12,2,384]{3,2,1,0:T(2,128)S(1)}, u32[]{:S(2)}, u32[]{:S(2)}) collective-permute-start(f32[3,12,2,384]{3,2,1,0:T(2,128)S(1)} %get-tuple-element.28), channel_id=1, source_target_pairs={{1,0},{2,1},{3,2},{4,3},{5,4},{6,5},{7,6},{8,7},{9,8},{10,9},{11,1... | collective-permute-start | bytes 331784 | tf_op jit(solution)/shard_map/ppermute | solution.py:25
  20.0 2.9 %collective-permute-start.2 = (f32[3,12,2,384]{3,2,1,0:T(2,128)S(1)}, f32[3,12,2,384]{3,2,1,0:T(2,128)S(1)}, u32[]{:S(2)}, u32[]{:S(2)}) collective-permute-start(f32[3,12,2,384]{3,2,1,0:T(2,128)S(1)} %get-tuple-element.27), channel_id=1, source_target_pairs={{0,1},{1,2},{2,3},{3,4},{4,5},{5,6},{6,7},{7,8},{8,9},{9,10},{10,1... | collective-permute-start | bytes 331784 | tf_op jit(solution)/shard_map/ppermute | solution.py:24
  22.9 0.1 fusion.58
  23.0 2.1 %collective-permute-done.3 = f32[3,12,2,384]{3,2,1,0:T(2,128)S(1)} collective-permute-done((f32[3,12,2,384]{3,2,1,0:T(2,128)S(1)}, f32[3,12,2,384]{3,2,1,0:T(2,128)S(1)}, u32[]{:S(2)}, u32[]{:S(2)}) %collective-permute-start.3) | collective-permute-done | bytes 110624 | tf_op jit(solution)/shard_map/ppermute | solution.py:25
  25.1 0.0 collective-permute-done.2
  25.1 0.3 pad_maximum_fusion
  25.4 0.3 fusion.15
  25.7 0.3 fusion.18
  25.9 0.5 fusion.16
  26.5 0.4 fusion.22
  26.9 0.1 multiply_dynamic-update-slice_fusion.8
  27.0 1.3 %fusion.12 = (f32[3,10,34,384]{3,2,1,0:T(8,128)S(1)}, f32[3,10,34,384]{3,2,1,0:T(8,128)S(1)}) fusion(f32[3,10,34,384]{3,2,1,0:T(8,128)S(1)} %get-tuple-element.22, f32[384]{0:T(512)S(1)} %get-tuple-element.9, f32[3,12,32,384]{3,2,1,0:T(8,128)S(1)} %constant_dynamic-update-slice_fusion, f32[3,12,2,384]{3,2,1,0:T(2,128)S(1)} %collective-permute-done.2, ...), kind=kLoop, calls=%fused_computation.27 | loop fusion | flops 2350080 | bytes 6692352 | tf_op jit(solution)/shard_map/div | solution.py:36
  28.3 0.6 fusion.29
  29.0 0.1 multiply_dynamic-update-slice_fusion.1
  29.1 0.1 multiply_dynamic-update-slice_fusion
  29.2 0.3 broadcast_multiply_fusion
  29.5 0.4 fusion
  29.9 0.7 fusion.21
  30.7 0.4 fusion.36
  31.3 0.1 multiply_dynamic-update-slice_fusion.14
  31.4 0.1 multiply_dynamic-update-slice_fusion.13
  31.5 0.1 multiply_dynamic-update-slice_fusion.12
  31.5 0.1 multiply_dynamic-update-slice_fusion.7
  31.6 0.1 multiply_dynamic-update-slice_fusion.6
  31.7 0.1 multiply_dynamic-update-slice_fusion.5
  31.8 0.1 multiply_dynamic-update-slice_fusion.4
  31.9 0.1 multiply_dynamic-update-slice_fusion.3
  32.0 0.4 fusion.2
  32.4 0.9 %fusion.9 = f32[6,8,32,384]{3,2,1,0:T(8,128)S(1)} fusion(f32[6,8,32,384]{3,2,1,0:T(8,128)S(1)} %multiply_dynamic-update-slice_fusion.12, f32[6,8,34,384]{3,2,1,0:T(8,128)S(1)} %fusion.2), kind=kLoop, calls=%fused_computation.21 | loop fusion | flops 3538944 | bytes 11796480 | tf_op jit(solution)/shard_map/sub | solution.py:81
  33.3 0.9 %fusion.6 = f32[6,8,32,384]{3,2,1,0:T(8,128)S(1)} fusion(f32[6,8,34,384]{3,2,1,0:T(8,128)S(1)} %fusion, f32[6,8,32,384]{3,2,1,0:T(8,128)S(1)} %multiply_dynamic-update-slice_fusion.9, f32[8,32,384]{2,1,0:T(8,128)S(1)} %get-tuple-element.19, f32[384]{0:T(512)S(1)} %get-tuple-element.8), kind=kLoop, calls=%fused_computation.15 | loop fusion | flops 4718592 | bytes 12191232 | tf_op jit(solution)/shard_map/mul | solution.py:82
  34.2 1.4 %fusion.65 = (f32[384]{0:T(512)S(1)}, f32[8,32,384]{2,1,0:T(8,128)}, f32[384]{0:T(512)S(1)}, f32[8,32,384]{2,1,0:T(8,128)}) fusion(f32[6,8,32,384]{3,2,1,0:T(8,128)S(1)} %fusion.6, f32[6,8,32,384]{3,2,1,0:T(8,128)S(1)} %fusion.9), kind=kLoop, calls=%fused_computation.156 | loop fusion | flops 2948352 | bytes 5508096 | tf_op jit(solution)/shard_map/reduce_sum | solution.py:114
  35.7 16.8 %psum.35 = f32[2,384]{1,0:T(2,128)S(1)} all-reduce(f32[2,384]{1,0:T(2,128)S(1)} %pad_maximum_fusion.3), channel_id=1, replica_groups=mesh['gx_0'=8,'gx_1'=2,'gz_0'=4,'gz_1'=2,'gz_2'=2] {'gx_0'}, use_global_device_ids=true, to_apply=%region_2.3 | all-reduce | flops 768 | bytes 6144 | tf_op jit(solution)/shard_map/psum | solution.py:31
  52.4 3.8 %psum.36 = f32[2,384]{1,0:T(2,128)S(1)} all-reduce(f32[2,384]{1,0:T(2,128)S(1)} %psum.35), channel_id=1, replica_groups=mesh['gx_0'=8,'gx_1'=2,'gz_0'=4,'gz_1'=2,'gz_2'=2] {'gx_1'}, use_global_device_ids=true, to_apply=%region_3.4 | all-reduce | flops 768 | bytes 6144 | tf_op jit(solution)/shard_map/psum | solution.py:31
  56.2 8.3 %psum.37 = f32[2,384]{1,0:T(2,128)S(1)} all-reduce(f32[2,384]{1,0:T(2,128)S(1)} %psum.36), channel_id=1, replica_groups=mesh['gx_0'=8,'gx_1'=2,'gz_0'=4,'gz_1'=2,'gz_2'=2] {'gz_0'}, use_global_device_ids=true, to_apply=%region_4.5 | all-reduce | flops 768 | bytes 6144 | tf_op jit(solution)/shard_map/psum | solution.py:31
  64.5 6.7 %psum.38 = f32[2,384]{1,0:T(2,128)S(1)} all-reduce(f32[2,384]{1,0:T(2,128)S(1)} %psum.37), channel_id=1, replica_groups=mesh['gx_0'=8,'gx_1'=2,'gz_0'=4,'gz_1'=2,'gz_2'=2] {'gz_1'}, use_global_device_ids=true, to_apply=%region_5.6 | all-reduce | flops 768 | bytes 6144 | tf_op jit(solution)/shard_map/psum | solution.py:31
  71.2 13.0 %psum.39 = f32[2,384]{1,0:T(2,128)S(1)} all-reduce(f32[2,384]{1,0:T(2,128)S(1)} %psum.38), channel_id=1, replica_groups=mesh['gx_0'=8,'gx_1'=2,'gz_0'=4,'gz_1'=2,'gz_2'=2] {'gz_2'}, use_global_device_ids=true, to_apply=%region_6.7 | all-reduce | flops 768 | bytes 6144 | tf_op jit(solution)/shard_map/psum | solution.py:31
  84.2 0.0 copy-start.1
  84.3 1.1 %fusion.44 = f32[8,32,384]{2,1,0:T(8,128)} fusion(f32[10,34,384]{2,1,0:T(8,128)S(1)} %get-tuple-element.14, f32[10,34,384]{2,1,0:T(8,128)S(1)} %get-tuple-element.12, f32[10,34,384]{2,1,0:T(8,128)S(1)} %get-tuple-element.16, f32[10,34,384]{2,1,0:T(8,128)S(1)} %broadcast_multiply_fusion.1, f32[10,34,384]{2,1,0:T(8,128)S(1)} %bitcast.69, f32[384]{0:T(512)S(1)} %fusion.57), kind=kLoop, calls=%fused_computation.103 | loop fusion | flops 983040 | bytes 2360832 | tf_op jit(solution)/shard_map/mul | solution.py:117
  85.4 0.0 copy-done.1
  (21 shorter events, 0.6 us)
Async XLA Ops:
  0.6 15.4 %copy-start = (f32[3,8,32,384]{3,2,1,0:T(8,128)S(1)}, f32[3,8,32,384]{3,2,1,0:T(8,128)}, u32[]{:S(2)}) copy-start(f32[3,8,32,384]{3,2,1,0:T(8,128)} %param.2) | copy-start | bytes 3538948
  0.6 22.3 %copy-start.2 = (f32[385]{0:T(512)S(1)}, f32[385]{0:T(512)}, u32[]{:S(2)}) copy-start(f32[385]{0:T(512)} %param.3) | copy-start | bytes 4624
  1.8 14.2 %collective-permute-start = (f32[3,2,32,384]{3,2,1,0:T(8,128)S(1)}, f32[3,2,32,384]{3,2,1,0:T(8,128)S(1)}, u32[]{:S(2)}, u32[]{:S(2)}) collective-permute-start(f32[3,2,32,384]{3,2,1,0:T(8,128)S(1)} %get-tuple-element.30), channel_id=1, source_target_pairs={{0,16},{16,32},{32,48},{48,64},{64,80},{80,96},{96,112},{112,128},... | collective-permute-start | bytes 884744 | tf_op jit(solution)/shard_map/ppermute | solution.py:24
  3.9 13.9 %collective-permute-start.1 = (f32[3,2,32,384]{3,2,1,0:T(8,128)S(1)}, f32[3,2,32,384]{3,2,1,0:T(8,128)S(1)}, u32[]{:S(2)}, u32[]{:S(2)}) collective-permute-start(f32[3,2,32,384]{3,2,1,0:T(8,128)S(1)} %get-tuple-element.29), channel_id=1, source_target_pairs={{16,0},{32,16},{48,32},{64,48},{80,64},{96,80},{112,96},{128,112},... | collective-permute-start | bytes 884744 | tf_op jit(solution)/shard_map/ppermute | solution.py:25
  18.0 7.1 %collective-permute-start.3 = (f32[3,12,2,384]{3,2,1,0:T(2,128)S(1)}, f32[3,12,2,384]{3,2,1,0:T(2,128)S(1)}, u32[]{:S(2)}, u32[]{:S(2)}) collective-permute-start(f32[3,12,2,384]{3,2,1,0:T(2,128)S(1)} %get-tuple-element.28), channel_id=1, source_target_pairs={{1,0},{2,1},{3,2},{4,3},{5,4},{6,5},{7,6},{8,7},{9,8},{10,9},{11,1... | collective-permute-start | bytes 331784 | tf_op jit(solution)/shard_map/ppermute | solution.py:25
  20.0 5.1 %collective-permute-start.2 = (f32[3,12,2,384]{3,2,1,0:T(2,128)S(1)}, f32[3,12,2,384]{3,2,1,0:T(2,128)S(1)}, u32[]{:S(2)}, u32[]{:S(2)}) collective-permute-start(f32[3,12,2,384]{3,2,1,0:T(2,128)S(1)} %get-tuple-element.27), channel_id=1, source_target_pairs={{0,1},{1,2},{2,3},{3,4},{4,5},{5,6},{6,7},{7,8},{8,9},{9,10},{10,1... | collective-permute-start | bytes 331784 | tf_op jit(solution)/shard_map/ppermute | solution.py:24
  84.2 1.2 %copy-start.1 = (f32[384]{0:T(512)}, f32[384]{0:T(512)S(1)}, u32[]{:S(2)}) copy-start(f32[384]{0:T(512)S(1)} %fusion.61) | copy-start | bytes 4612
where the time goes:
time: 85.6 us; the launch traced here: 85.4 us
  blocking collectives  48.5 us (57%)
  starting transfers between devices  12.4 us (14%)
  other arithmetic  11.4 us (13%)
  waiting for transfers between devices  10.5 us (12%)
  local copies, waits for them, and re-layouts  1.59 us (2%)
  between operations  0.96 us (1%)
    psum x5, blocking collectives, over_axes(): return functools.reduce(lax.psum, axes, array)  48.5 us
    ppermute x2, starting transfers between devices, extended(): after = lax.ppermute(leading, axis, down)  7.43 us
    ppermute x2, waiting for transfers between devices, extended(): before = lax.ppermute(last, axis, up)  6.67 us
    ppermute x2, starting transfers between devices, extended(): before = lax.ppermute(last, axis, up)  5.01 us
    ppermute x2, waiting for transfers between devices, extended(): after = lax.ppermute(leading, axis, down)  3.8 us
    div x2, other arithmetic, wall_slope(): return (padded[..., 2:] - padded[..., :-2]) / (y_gap[:-1] + y_gap[1:])  1.94 us
  transfers between devices with their start and end apart: 4, of which 3 were waited for; matrix products, arithmetic and copies ran while one was open for 0% of the time, Pallas kernels for 0%

commit v1 on v0

v1 whole, which is shorter than its diff:
```python
import jax
import jax.numpy as jnp
from jax import lax
from jax.experimental import pallas as pl
from jax.experimental.pallas import tpu as pltpu
from jax.sharding import Mesh
from jax.sharding import PartitionSpec as P

AXES = ("gx_0", "gx_1", "gz_0", "gz_1", "gz_2")
GX = ("gx_0", "gx_1")
GZ = ("gz_0", "gz_1", "gz_2")
MESH = pl.DeviceIdType.MESH

LANES = 128
ROWS = 8
TINY = 1.1754944e-38
ORDER = (0, 3, 1, 2)


def root(square):
    return square * lax.rsqrt(jnp.maximum(square, TINY))


def kernel(sizes, planes, vel, gaps, eddy, lm_out, mm_out, coef_out, pad, field, acc, sent, plane_in, line_in,
           load_sem, send_sem, recv_sem, plane_send, plane_recv, line_send, line_recv):
    nz, nxl, ny, nxh, nc = sizes
    nx, depth = vel.shape[1], vel.shape[2]
    chunks = vel.shape[3] // LANES
    tiles = depth // ROWS
    me = tuple(lax.axis_index(name) for name in AXES)

    loads = []
    for part in range(3):
        for chunk in range(chunks):
            loads.append(
                pltpu.make_async_copy(
                    vel.at[part, :, :, pl.ds(chunk * LANES, LANES)],
                    pad.at[part, chunk, pl.ds(2, nx), pl.ds(2, depth), :],
                    load_sem.at[part * chunks + chunk],
                )
            )
    for load in loads:
        load.start()

    def along_x(step):
        ring = nz * nxl
        spot = lax.rem(me[0] * nxl + me[1] + step + ring, ring)
        return (spot // nxl, lax.rem(spot, nxl), me[2], me[3], me[4])

    def along_z(step):
        ring = ny * nxh * nc
        spot = lax.rem((me[2] * nxh + me[3]) * nc + me[4] + step + ring, ring)
        return (me[0], me[1], spot // (nxh * nc), lax.rem(spot // nc, nxh), lax.rem(spot, nc))

    plane = [(a, b, c, d) for a in range(nxl) for b in range(ny) for c in range(nxh) for d in range(nc)]

    def in_plane(off, sign):
        step = [lax.rem(m + sign * o + n, n) for m, o, n in zip(me[1:], off, (nxl, ny, nxh, nc))]
        return (me[0], *step)

    def plane_slot(spot):
        return ((spot[1] * ny + spot[2]) * nxh + spot[3]) * nc + spot[4]

    def on_line(off, sign):
        return (lax.rem(me[0] + sign * off + nz, nz), *me[1:])

    barrier = pltpu.get_barrier_semaphore()
    outside = jnp.where(me[1] == nxl - 1, 1, -1)
    greeted = [along_x(outside)] + [in_plane(off, 1) for off in plane[1:]] + [on_line(off, 1) for off in range(1, nz)]
    for other in greeted:
        pl.semaphore_signal(barrier, inc=1, device_id=other, device_id_type=MESH)
    acc[...] = jnp.zeros_like(acc)
    pl.semaphore_wait(barrier, len(greeted))
    for load in loads:
        load.wait()

    def rim(number, source, target, other):
        return pltpu.make_async_remote_copy(
            src_ref=pad.at[:, :, pl.ds(*source[0]), pl.ds(*source[1]), :],
            dst_ref=pad.at[:, :, pl.ds(*target[0]), pl.ds(*target[1]), :],
            send_sem=send_sem.at[number],
            recv_sem=recv_sem.at[number],
            device_id=other,
            device_id_type=MESH,
        )

    up, down, right, left = along_x(1), along_x(-1), along_z(1), along_z(-1)
    body = (2, nx)
    sides = [
        rim(0, (body, (depth, 2)), (body, (0, 2)), right),
        rim(1, (body, (2, 2)), (body, (depth + 2, 2)), left),
    ]
    strips = []
    for tile in range(tiles):
        cut = (2 + ROWS * tile, ROWS)
        strips.append((
            rim(2 + 2 * tile, ((nx, 2), cut), ((0, 2), cut), up),
            rim(3 + 2 * tile, ((2, 2), cut), ((nx + 2, 2), cut), down),
        ))
    first = 2 + 2 * tiles
    ends = [(0, 2), (nx + 2, 2)]
    corners_left = [rim(first + k, (end, (2, 2)), (end, (depth + 2, 2)), left) for k, end in enumerate(ends)]
    corners_right = [rim(first + 2 + k, (end, (depth, 2)), (end, (0, 2)), right) for k, end in enumerate(ends)]

    for side in sides:
        side.start()
    for tile in ORDER:
        for strip in strips[tile]:
            strip.start()

    lane = lax.broadcasted_iota(jnp.int32, (ROWS, LANES), 1)
    low, high = lane == 0, lane == LANES - 1
    zero = jnp.zeros((ROWS, LANES), jnp.float32)

    def strains(row, tile):
        here, at = row + 2, ROWS * tile + 1

        def speed(part, chunk, dx=0, dz=0):
            return pad[part, chunk, here + dx, pl.ds(at + dz, ROWS), :]

        middle = [[speed(part, chunk) for chunk in range(chunks)] for part in range(3)]
        before = [[pltpu.roll(v, 1, 1) for v in parts] for parts in middle]
        after = [[pltpu.roll(v, LANES - 1, 1) for v in parts] for parts in middle]
        for chunk in range(chunks):
            rate = jnp.broadcast_to(gaps[0:1, pl.ds(chunk * LANES, LANES)], (ROWS, LANES))

            def slope_y(part):
                upper = jnp.where(high, after[part][chunk + 1] if chunk + 1 < chunks else zero, after[part][chunk])
                lower = jnp.where(low, before[part][chunk - 1] if chunk else zero, before[part][chunk])
                return (upper - lower) * rate

            def slope_x(part):
                return speed(part, chunk, dx=1) - speed(part, chunk, dx=-1)

            def slope_z(part):
                return speed(part, chunk, dz=1) - speed(part, chunk, dz=-1)

            strain = [
                slope_x(0),
                slope_y(1),
                slope_z(2),
                slope_y(0) + slope_x(1),
                slope_z(0) + slope_x(2),
                slope_z(1) + slope_y(2),
            ]
            ours = [middle[part][chunk] for part in range(3)]
            square = [s * s for s in strain]
            size = root(0.5 * (square[0] + square[1] + square[2]) + 0.25 * (square[3] + square[4] + square[5]))
            pairs = [ours[0] * ours[0], ours[1] * ours[1], ours[2] * ours[2],
                     ours[0] * ours[1], ours[0] * ours[2], ours[1] * ours[2]]
            values = strain + [size * s for s in strain] + pairs + ours + [size]
            for number, value in enumerate(values):
                field[number, chunk, row + 1, pl.ds(ROWS * tile, ROWS), :] = value

    def model(row, tile):
        for chunk in range(chunks):
            def smooth(number):
                lines = []
                for k in range(4):
                    a, b, c = (field[number, chunk, row + k, pl.ds(ROWS * tile + dz, ROWS), :] for dz in range(3))
                    lines.append((a + c) + (b + b))
                pair = [lines[k] + lines[k + 1] for k in range(3)]
                return [pair[k] + pair[k + 1] for k in range(2)]

            test = [smooth(k) for k in range(6)]
            speeds = [[0.25 * s for s in smooth(18 + k)] for k in range(3)]
            scale = []
            for k in range(2):
                t = [v[k] * v[k] for v in test]
                scale.append(root((1.0 / 32.0) * (t[0] + t[1] + t[2]) + (1.0 / 64.0) * (t[3] + t[4] + t[5])))
            lm, mm_d, mm_o = [zero, zero], [zero, zero], [zero, zero]
            for number, (i, j) in enumerate(((0, 0), (1, 1), (2, 2), (0, 1), (0, 2), (1, 2))):
                stress, pairs = smooth(6 + number), smooth(12 + number)
                for k in range(2):
                    term = stress[k] - scale[k] * test[number][k]
                    lm[k] = lm[k] + (pairs[k] - speeds[i][k] * speeds[j][k]) * term
                    if number < 3:
                        mm_d[k] = mm_d[k] + term * term
                    else:
                        mm_o[k] = mm_o[k] + term * term
            lm_scale = jnp.broadcast_to(gaps[1:2, pl.ds(chunk * LANES, LANES)], (ROWS, LANES))
            mm_scale = jnp.broadcast_to(gaps[2:3, pl.ds(chunk * LANES, LANES)], (ROWS, LANES))
            lm = [lm_scale * v for v in lm]
            mm = [mm_scale * (a + 0.5 * b) for a, b in zip(mm_d, mm_o)]
            for k in range(2):
                spot = (row + k, pl.ds(ROWS * tile, ROWS), pl.ds(chunk * LANES, LANES))
                lm_out[spot] = lm[k]
                mm_out[spot] = mm[k]
            acc[chunk] += lm[0] + lm[1]
            acc[chunks + chunk] += mm[0] + mm[1]

    def over(start, stop, call, step=1):
        def turn(k, carry):
            call(start + step * k)
            return carry
        lax.fori_loop(0, (stop - start) // step, turn, 0)

    for tile in range(1, tiles - 1):
        over(1, nx - 1, lambda row, tile=tile: strains(row, tile))
    for side in sides:
        side.wait_recv()
    for tile in (0, tiles - 1, tiles):
        over(1, nx - 1, lambda row, tile=tile: strains(row, tile))
    for tile in range(tiles):
        over(2, nx - 2, lambda row, tile=tile: model(row, tile), step=2)

    edges = ((-1, 0), (nx - 1, nx))

    def edge_strains(tile):
        for pair in edges:
            over(pair[0], pair[1] + 1, lambda row: strains(row, tile))

    def edge_model(tile):
        over(0, 2 * (nx - 2), lambda row: model(row, tile), step=nx - 2)

    for strip in strips[0]:
        strip.wait_recv()
    for corner in corners_left:
        corner.start()
    for strip in strips[tiles - 1]:
        strip.wait_recv()
    for corner in corners_right:
        corner.start()
    for strip in strips[1]:
        strip.wait_recv()
    edge_strains(1)
    for corner in corners_left + corners_right:
        corner.wait_recv()
    edge_strains(0)
    edge_strains(tiles)
    edge_model(0)
    for strip in strips[2]:
        strip.wait_recv()
    edge_strains(2)
    edge_strains(3)
    for tile in range(1, tiles):
        edge_model(tile)

    for number in range(2 * chunks):
        sent[0, number : number + 1, :] = jnp.sum(acc[number], axis=0, keepdims=True)
    for number in range(2 * chunks, ROWS):
        sent[0, number : number + 1, :] = jnp.zeros((1, LANES), jnp.float32)
    mine = plane_slot(me)
    plane_in[mine] = sent[0]
    copies = []
    for number, off in enumerate(plane[1:]):
        copy = pltpu.make_async_remote_copy(
            src_ref=sent.at[0], dst_ref=plane_in.at[mine],
            send_sem=plane_send.at[number], recv_sem=plane_recv.at[mine],
            device_id=in_plane(off, 1), device_id_type=MESH,
        )
        copy.start()
        copies.append(copy)
    for off in plane[1:]:
        slot = plane_slot(in_plane(off, -1))
        pltpu.make_async_remote_copy(
            src_ref=sent.at[0], dst_ref=plane_in.at[slot],
            send_sem=plane_send.at[0], recv_sem=plane_recv.at[slot],
            device_id=in_plane(off, -1), device_id_type=MESH,
        ).wait_recv()
    total = [plane_in[k] for k in range(len(plane))]
    while len(total) > 1:
        total = [a + b for a, b in zip(total[::2], total[1::2])]
    sent[1] = total[0]
    line_in[me[0]] = total[0]
    for off in range(1, nz):
        copy = pltpu.make_async_remote_copy(
            src_ref=sent.at[1], dst_ref=line_in.at[me[0]],
            send_sem=line_send.at[off], recv_sem=line_recv.at[me[0]],
            device_id=on_line(off, 1), device_id_type=MESH,
        )
        copy.start()
        copies.append(copy)
    for off in range(1, nz):
        slot = on_line(off, -1)[0]
        pltpu.make_async_remote_copy(
            src_ref=sent.at[1], dst_ref=line_in.at[slot],
            send_sem=line_send.at[off], recv_sem=line_recv.at[slot],
            device_id=on_line(off, -1), device_id_type=MESH,
        ).wait_recv()
    total = [line_in[k] for k in range(nz)]
    while len(total) > 1:
        total = [a + b for a, b in zip(total[::2], total[1::2])]
    total = total[0]

    factors = []
    for chunk in range(chunks):
        number = pl.ds(chunk * LANES, LANES)
        share = total[chunk : chunk + 1, :] * (1.0 / planes)
        base = total[chunks + chunk : chunks + chunk + 1, :] * (1.0 / planes) + 1e-06
        coefficient = share / base
        coef_out[0:1, number] = coefficient
        factors.append(jnp.broadcast_to(coefficient * gaps[3:4, number], (ROWS, LANES)))

    def viscosity(row):
        for tile in range(tiles):
            for chunk in range(chunks):
                size = field[21, chunk, row + 1, pl.ds(ROWS * tile + 1, ROWS), :]
                eddy[row, pl.ds(ROWS * tile, ROWS), pl.ds(chunk * LANES, LANES)] = factors[chunk] * size

    over(0, nx, viscosity)
    for copy in sides + [s for pair in strips for s in pair] + corners_left + corners_right + copies:
        copy.wait_send()


def solution(mesh):
    shape = (8, 2, 4, 2, 2)
    torus = Mesh(mesh.devices.reshape(shape), AXES)

    def per_device(velocity, y_gap):
        _, nx, depth, height = velocity.shape
        chunks, tiles = height // LANES, depth // ROWS
        cells = nx * lax.axis_size(GX) * depth * lax.axis_size(GZ)
        span = y_gap[:-1] + y_gap[1:]
        width_sq = (0.5 * span) ** (2.0 / 3.0)
        gaps = jnp.stack([2.0 / span, width_sq * (1.0 / 256.0), width_sq * width_sq * (1.0 / 256.0), width_sq])
        rims = 2 + 2 * tiles + 4
        in_plane = shape[1] * shape[2] * shape[3] * shape[4]
        grid = jax.ShapeDtypeStruct((nx, depth, height), jnp.float32)
        vmem = pl.BlockSpec(memory_space=pltpu.VMEM)
        eddy, lm, mm, coefficient = pl.pallas_call(
            lambda *refs: kernel(shape, cells, *refs),
            out_shape=(grid, grid, grid, jax.ShapeDtypeStruct((1, height), jnp.float32)),
            in_specs=[pl.BlockSpec(memory_space=pltpu.HBM), vmem],
            out_specs=(vmem, vmem, vmem, vmem),
            scratch_shapes=[
                pltpu.VMEM((3, chunks, nx + 4, depth + 16, LANES), jnp.float32),
                pltpu.VMEM((22, chunks, nx + 2, depth + 8, LANES), jnp.float32),
                pltpu.VMEM((2 * chunks, ROWS, LANES), jnp.float32),
                pltpu.VMEM((2, ROWS, LANES), jnp.float32),
                pltpu.VMEM((in_plane, ROWS, LANES), jnp.float32),
                pltpu.VMEM((shape[0], ROWS, LANES), jnp.float32),
                pltpu.SemaphoreType.DMA((3 * chunks,)),
                pltpu.SemaphoreType.DMA((rims,)),
                pltpu.SemaphoreType.DMA((rims,)),
                pltpu.SemaphoreType.DMA((in_plane,)),
                pltpu.SemaphoreType.DMA((in_plane,)),
                pltpu.SemaphoreType.DMA((shape[0],)),
                pltpu.SemaphoreType.DMA((shape[0],)),
            ],
            compiler_params=pltpu.CompilerParams(
                collective_id=0, has_side_effects=True, vmem_limit_bytes=40 * 1024 * 1024
            ),
            name="smagorinsky",
        )(velocity, gaps)
        return eddy, lm, mm, coefficient[0]

    return jax.shard_map(
        per_device,
        mesh=torus,
        in_specs=(P(None, GX, GZ, None), P()),
        out_specs=(P(GX, GZ, None), P(GX, GZ, None), P(GX, GZ, None), P()),
        check_vma=False,
    )
```

time: 85.6 us -> 48 us (0.56)
  blocking collectives: 48.5 us -> 0 us
  Pallas kernels: 0 us -> 42.2 us
  starting transfers between devices: 12.4 us -> 0 us
  waiting for transfers between devices: 10.5 us -> 0 us
  other arithmetic: 11.4 us -> 1.47 us
  local copies, waits for them, and re-layouts: 1.59 us -> 3.51 us
    psum x5 -> x0, blocking collectives: 48.5 us -> none  [over_axes(): return functools.reduce(lax.psum, axes, array)]
    pallas_call x0 -> x1, Pallas kernels: none -> 42.2 us  [per_device(): pl.pallas_call(lambda *refs: kernel(shape, cells, *refs), out_shape=(grid...]
    ppermute x4 -> x0, starting transfers between devices: 12.4 us -> none  [the longest x2 7.43 us: extended(): after = lax.ppermute(leading, axis, down)]
    ppermute x4 -> x0, waiting for transfers between devices: 10.5 us -> none  [the longest x2 6.67 us: extended(): before = lax.ppermute(last, axis, up)]
    mul x10 -> x2, other arithmetic: 4.09 us -> 0.86 us  [the longest x1 0.85 us: per_device(): width_sq * (1.0 / 256.0)]
    unnamed x13 -> x5, local copies, waits for them, and re-layouts: 0.29 us -> 3.5 us
    div x3 -> x0, other arithmetic: 1.97 us -> none  [the longest x2 1.94 us: wall_slope(): return (padded[..., 2:] - padded[..., :-2]) / (y_gap[:-1] + y_gap[1:])]
    add x4 -> x0, other arithmetic: 1.61 us -> none  [the longest x3 1.07 us: rim_filter(): 0.25 * values[:, :-2] + 0.5 * values[:, 1:-1] + 0.25 * values[:, 2:]]
  transfers between devices with their start and end apart: 4 -> 0, of which waited for: 3 -> 0; matrix products, arithmetic and copies ran while one was open for 0% -> 0% of each run, Pallas kernels for 0% -> 0%
where the time goes in v1:
time: 48 us; the launch traced here: 47.9 us
  Pallas kernels  42.2 us (88%)
  local copies, waits for them, and re-layouts  3.51 us (7%)
  other arithmetic  1.47 us (3%)
  between operations  0.69 us (1%)
    pallas_call x1, Pallas kernels, per_device(): pl.pallas_call(lambda *refs: kernel(shape, cells, *refs), out_shape=(grid...  42.2 us
    unnamed x5, local copies, waits for them, and re-layouts  3.5 us

profile of v1, /device:TPU:1, one launch (start us, length us, event | category | flops | bytes accessed | tf_op | source)
XLA Modules:
  0.0 47.9 jit_solution(10149882088557402039)
XLA Ops:
  0.6 0.9 %broadcast_multiply_fusion = (f32[384]{0:T(512)S(1)}, f32[384]{0:T(512)S(1)}, f32[384]{0:T(512)S(1)}) fusion(f32[385]{0:T(512)} %param.3), kind=kLoop, calls=%fused_computation.4 | loop fusion | flops 1536 | bytes 7680 | tf_op jit(solution)/shard_map/mul | solution.py:316
  1.6 0.0 copy-start
  1.6 1.3 %copy-done = f32[3,8,32,384]{3,2,1,0:T(8,128)S(1)} copy-done((f32[3,8,32,384]{3,2,1,0:T(8,128)S(1)}, f32[3,8,32,384]{3,2,1,0:T(8,128)}, u32[]{:S(2)}) %copy-start) | copy-done | bytes 1179672
  2.8 42.2 %smagorinsky.1 = (f32[8,32,384]{2,1,0:T(8,128)S(1)}, f32[8,32,384]{2,1,0:T(8,128)S(1)}, f32[8,32,384]{2,1,0:T(8,128)S(1)}, f32[1,384]{1,0:T(1,128)S(1)}) custom-call(f32[3,8,32,384]{3,2,1,0:T(8,128)S(1)} %copy-done, f32[4,384]{1,0:T(4,128)S(1)} %pad_maximum_fusion.refs_1_), custom_call_target="tpu_custom_call" | custom-call | tf_op jit(solution)/shard_map/smagorinsky/pallas_call | solution.py:321
  45.0 0.6 %reduce = f32[384]{0:T(512)} reduce(f32[1,384]{1,0:T(1,128)S(1)} %get-tuple-element.11, f32[]{:T(128)} %constant.9), dimensions={0}, to_apply=%get-tuple-element.11.reduce_sub_computation | reduce | bytes 3076 | tf_op jit(solution)/shard_map/smagorinsky/pallas_call | solution.py:321
  45.6 0.7 %copy.9 = f32[8,32,384]{2,1,0:T(8,128)} copy(f32[8,32,384]{2,1,0:T(8,128)S(1)} %get-tuple-element.19) | data formatting | bytes 786432
  46.4 0.7 %copy.10 = f32[8,32,384]{2,1,0:T(8,128)} copy(f32[8,32,384]{2,1,0:T(8,128)S(1)} %get-tuple-element.20) | data formatting | bytes 786432
  47.1 0.7 %copy.11 = f32[8,32,384]{2,1,0:T(8,128)} copy(f32[8,32,384]{2,1,0:T(8,128)S(1)} %get-tuple-element.21) | data formatting | bytes 786432
  (6 shorter events, 0.0 us)
Async XLA Ops:
  1.6 1.3 %copy-start = (f32[3,8,32,384]{3,2,1,0:T(8,128)S(1)}, f32[3,8,32,384]{3,2,1,0:T(8,128)}, u32[]{:S(2)}) copy-start(f32[3,8,32,384]{3,2,1,0:T(8,128)} %refs_0_.1) | copy-start | bytes 3538948

commit v2 on v1

v2 whole, which is shorter than its diff:
```python
import jax
import jax.numpy as jnp
from jax import lax
from jax.experimental import pallas as pl
from jax.experimental.pallas import tpu as pltpu
from jax.sharding import Mesh
from jax.sharding import PartitionSpec as P

AXES = ("gx_0", "gx_1", "gz_0", "gz_1", "gz_2")
GX = ("gx_0", "gx_1")
GZ = ("gz_0", "gz_1", "gz_2")
MESH = pl.DeviceIdType.MESH

LANES = 128
ROWS = 8
TINY = 1.1754944e-38


def root(square):
    return square * lax.rsqrt(jnp.maximum(square, TINY))


def kernel(sizes, planes, vel, y_gap, size_out, lm_out, mm_out, coef_out, pad, field, gap, last, gaps, acc, sent, got,
           load_sem, send_sem, recv_sem, sum_send, sum_recv):
    nz, nxl, ny, nxh, nc = sizes
    nx, depth = vel.shape[1], vel.shape[2]
    chunks = vel.shape[3] // LANES
    tiles = depth // ROWS
    me = tuple(lax.axis_index(name) for name in AXES)

    loads = []
    for part in range(3):
        for chunk in range(chunks):
            loads.append(
                pltpu.make_async_copy(
                    vel.at[part, :, :, pl.ds(chunk * LANES, LANES)],
                    pad.at[part, chunk, pl.ds(2, nx), pl.ds(2, depth), :],
                    load_sem.at[part * chunks + chunk],
                )
            )
    loads.append(pltpu.make_async_copy(y_gap.at[pl.ds(0, chunks * LANES)], gap, load_sem.at[3 * chunks]))
    loads.append(pltpu.make_async_copy(y_gap, last, load_sem.at[3 * chunks + 1]))

    def along_x(step):
        ring = nz * nxl
        spot = lax.rem(me[0] * nxl + me[1] + step + ring, ring)
        return (spot // nxl, lax.rem(spot, nxl), me[2], me[3], me[4])

    def along_z(step):
        ring = ny * nxh * nc
        spot = lax.rem((me[2] * nxh + me[3]) * nc + me[4] + step + ring, ring)
        return (me[0], me[1], spot // (nxh * nc), lax.rem(spot // nc, nxh), lax.rem(spot, nc))

    def around(gx_step, gz_step):
        z, xl, *_ = along_x(gx_step)
        return (z, xl, *along_z(gz_step)[2:])

    def near(off, sign):
        xl, xh, c = (lax.rem(m + sign * o + n, n) for m, o, n in zip((me[1], me[3], me[4]), off, (nxl, nxh, nc)))
        return (me[0], xl, me[2], xh, c)

    def on_y(off, sign):
        return (me[0], me[1], lax.rem(me[2] + sign * off + ny, ny), me[3], me[4])

    def on_z(off, sign):
        return (lax.rem(me[0] + sign * off + nz, nz), *me[1:])

    group = [(a, b, c) for a in range(nxl) for b in range(nxh) for c in range(nc)]
    stages = (
        (near, group[1:], lambda spot: (spot[1] * nxh + spot[3]) * nc + spot[4], len(group)),
        (on_y, range(1, ny), lambda spot: spot[2], ny),
        (on_z, range(1, nz), lambda spot: spot[0], nz),
    )

    barrier = pltpu.get_barrier_semaphore()
    steps = [(1, 0), (-1, 0), (0, 1), (0, -1), (1, 1), (1, -1), (-1, 1), (-1, -1)]
    greeted = [around(*step) for step in steps] + [to(off, 1) for to, offs, _, _ in stages for off in offs]
    for other in greeted:
        pl.semaphore_signal(barrier, inc=1, device_id=other, device_id_type=MESH)
    for load in loads:
        load.start()
    acc[...] = jnp.zeros_like(acc)
    for load in loads:
        load.wait()
    pl.semaphore_wait(barrier, len(greeted))

    def rim(number, source, target, other):
        return pltpu.make_async_remote_copy(
            src_ref=pad.at[:, :, pl.ds(*source[0]), pl.ds(*source[1]), :],
            dst_ref=pad.at[:, :, pl.ds(*target[0]), pl.ds(*target[1]), :],
            send_sem=send_sem.at[number],
            recv_sem=recv_sem.at[number],
            device_id=other,
            device_id_type=MESH,
        )

    up, down, right, left = along_x(1), along_x(-1), along_z(1), along_z(-1)
    body = (2, nx)
    sides = [
        rim(0, (body, (depth, 2)), (body, (0, 2)), right),
        rim(1, (body, (2, 2)), (body, (depth + 2, 2)), left),
    ]
    strips = []
    for tile in range(tiles):
        cut = (2 + ROWS * tile, ROWS)
        strips.append((
            rim(2 + 2 * tile, ((nx, 2), cut), ((0, 2), cut), up),
            rim(3 + 2 * tile, ((2, 2), cut), ((nx + 2, 2), cut), down),
        ))
    first = 2 + 2 * tiles
    corners = [
        rim(first, ((nx, 2), (depth, 2)), ((0, 2), (0, 2)), around(1, 1)),
        rim(first + 1, ((nx, 2), (2, 2)), ((0, 2), (depth + 2, 2)), around(1, -1)),
        rim(first + 2, ((2, 2), (depth, 2)), ((nx + 2, 2), (0, 2)), around(-1, 1)),
        rim(first + 3, ((2, 2), (2, 2)), ((nx + 2, 2), (depth + 2, 2)), around(-1, -1)),
    ]

    for copy in sides + corners + [strip for pair in strips for strip in pair]:
        copy.start()

    lane = lax.broadcasted_iota(jnp.int32, (ROWS, LANES), 1)
    low, high = lane == 0, lane == LANES - 1
    zero = jnp.zeros((ROWS, LANES), jnp.float32)
    for chunk in range(chunks):
        line = pl.ds(chunk * LANES, LANES)
        here = gap[line].reshape(1, LANES)
        if chunk + 1 < chunks:
            then = gap[pl.ds((chunk + 1) * LANES, LANES)].reshape(1, LANES)
        else:
            then = last[chunks * LANES]
        after = pltpu.roll(jnp.where(low[:1], then, here), LANES - 1, 1)
        span = here + after
        width_sq = jnp.exp((2.0 / 3.0) * jnp.log(0.5 * span))
        gaps[0:1, line] = 2.0 / span
        gaps[1:2, line] = width_sq * (1.0 / 256.0)
        gaps[2:3, line] = width_sq * width_sq * (1.0 / 256.0)
        gaps[3:4, line] = width_sq

    def strains(row, tile):
        here, at = row + 2, ROWS * tile + 1

        def speed(part, chunk, dx=0, dz=0):
            return pad[part, chunk, here + dx, pl.ds(at + dz, ROWS), :]

        middle = [[speed(part, chunk) for chunk in range(chunks)] for part in range(3)]
        before = [[pltpu.roll(v, 1, 1) for v in parts] for parts in middle]
        after = [[pltpu.roll(v, LANES - 1, 1) for v in parts] for parts in middle]
        for chunk in range(chunks):
            rate = jnp.broadcast_to(gaps[0:1, pl.ds(chunk * LANES, LANES)], (ROWS, LANES))

            def slope_y(part):
                upper = jnp.where(high, after[part][chunk + 1] if chunk + 1 < chunks else zero, after[part][chunk])
                lower = jnp.where(low, before[part][chunk - 1] if chunk else zero, before[part][chunk])
                return (upper - lower) * rate

            def slope_x(part):
                return speed(part, chunk, dx=1) - speed(part, chunk, dx=-1)

            def slope_z(part):
                return speed(part, chunk, dz=1) - speed(part, chunk, dz=-1)

            strain = [
                slope_x(0),
                slope_y(1),
                slope_z(2),
                slope_y(0) + slope_x(1),
                slope_z(0) + slope_x(2),
                slope_z(1) + slope_y(2),
            ]
            ours = [middle[part][chunk] for part in range(3)]
            square = [s * s for s in strain]
            size = root(0.5 * (square[0] + square[1] + square[2]) + 0.25 * (square[3] + square[4] + square[5]))
            pairs = [ours[0] * ours[0], ours[1] * ours[1], ours[2] * ours[2],
                     ours[0] * ours[1], ours[0] * ours[2], ours[1] * ours[2]]
            values = strain + [size * s for s in strain] + pairs + ours + [size]
            for number, value in enumerate(values):
                field[number, chunk, row + 1, pl.ds(ROWS * tile, ROWS), :] = value

    def model(row, tile):
        for chunk in range(chunks):
            def smooth(number):
                lines = []
                for k in range(4):
                    a, b, c = (field[number, chunk, row + k, pl.ds(ROWS * tile + dz, ROWS), :] for dz in range(3))
                    lines.append((a + c) + (b + b))
                pair = [lines[k] + lines[k + 1] for k in range(3)]
                return [pair[k] + pair[k + 1] for k in range(2)]

            test = [smooth(k) for k in range(6)]
            speeds = [[0.25 * s for s in smooth(18 + k)] for k in range(3)]
            scale = []
            for k in range(2):
                t = [v[k] * v[k] for v in test]
                scale.append(root((1.0 / 32.0) * (t[0] + t[1] + t[2]) + (1.0 / 64.0) * (t[3] + t[4] + t[5])))
            lm, mm_d, mm_o = [zero, zero], [zero, zero], [zero, zero]
            for number, (i, j) in enumerate(((0, 0), (1, 1), (2, 2), (0, 1), (0, 2), (1, 2))):
                stress, pairs = smooth(6 + number), smooth(12 + number)
                for k in range(2):
                    term = stress[k] - scale[k] * test[number][k]
                    lm[k] = lm[k] + (pairs[k] - speeds[i][k] * speeds[j][k]) * term
                    if number < 3:
                        mm_d[k] = mm_d[k] + term * term
                    else:
                        mm_o[k] = mm_o[k] + term * term
            lm_scale = jnp.broadcast_to(gaps[1:2, pl.ds(chunk * LANES, LANES)], (ROWS, LANES))
            mm_scale = jnp.broadcast_to(gaps[2:3, pl.ds(chunk * LANES, LANES)], (ROWS, LANES))
            lm = [lm_scale * v for v in lm]
            mm = [mm_scale * (a + 0.5 * b) for a, b in zip(mm_d, mm_o)]
            for k in range(2):
                spot = (row + k, pl.ds(ROWS * tile, ROWS), pl.ds(chunk * LANES, LANES))
                size_out[spot] = field[21, chunk, row + k + 1, pl.ds(ROWS * tile + 1, ROWS), :]
                lm_out[spot] = lm[k]
                mm_out[spot] = mm[k]
            acc[chunk] += lm[0] + lm[1]
            acc[chunks + chunk] += mm[0] + mm[1]

    def over(start, stop, call, step=1):
        def turn(k, carry):
            call(start + step * k)
            return carry
        lax.fori_loop(0, (stop - start) // step, turn, 0)

    for tile in range(1, tiles - 1):
        over(1, nx - 1, lambda row, tile=tile: strains(row, tile))
    for side in sides:
        side.wait_recv()
    for tile in (0, tiles - 1, tiles):
        over(1, nx - 1, lambda row, tile=tile: strains(row, tile))
    for tile in range(tiles):
        over(2, nx - 2, lambda row, tile=tile: model(row, tile), step=2)

    edges = ((-1, 0, 0), (nx - 1, nx - 1, nx - 2))
    for tile in range(tiles + 1):
        for side, (start, _, block) in enumerate(edges):
            if tile == 0:
                corners[2 * side].wait_recv()
                corners[2 * side + 1].wait_recv()
            if tile < tiles:
                strips[tile][side].wait_recv()
            over(start, start + 2, lambda row, tile=tile: strains(row, tile))
            if tile:
                model(block, tile - 1)

    for number in range(2 * chunks):
        sent[0, number : number + 1, :] = jnp.sum(acc[number], axis=0, keepdims=True)
    for number in range(2 * chunks, ROWS):
        sent[0, number : number + 1, :] = jnp.zeros((1, LANES), jnp.float32)
    total = sent[0]
    copies, base = [], 0
    for number, (to, offs, slot_of, count) in enumerate(stages):
        if number:
            sent[number] = total
        mine = base + slot_of(me)
        got[mine] = total
        for off in offs:
            copy = pltpu.make_async_remote_copy(
                src_ref=sent.at[number], dst_ref=got.at[mine],
                send_sem=sum_send.at[len(copies)], recv_sem=sum_recv.at[mine],
                device_id=to(off, 1), device_id_type=MESH,
            )
            copy.start()
            copies.append(copy)
        for off in offs:
            other = to(off, -1)
            slot = base + slot_of(other)
            pltpu.make_async_remote_copy(
                src_ref=sent.at[number], dst_ref=got.at[slot],
                send_sem=sum_send.at[0], recv_sem=sum_recv.at[slot],
                device_id=other, device_id_type=MESH,
            ).wait_recv()
        terms = [got[base + k] for k in range(count)]
        while len(terms) > 1:
            terms = [a + b for a, b in zip(terms[::2], terms[1::2])]
        total = terms[0]
        base += count

    for chunk in range(chunks):
        line = pl.ds(chunk * LANES, LANES)
        share = total[chunk : chunk + 1, :] * (1.0 / planes)
        below = total[chunks + chunk : chunks + chunk + 1, :] * (1.0 / planes) + 1e-06
        coefficient = share / below
        coef_out[0:1, line] = coefficient
        coef_out[1:2, line] = coefficient * gaps[3:4, line]
    for copy in sides + corners + [strip for pair in strips for strip in pair] + copies:
        copy.wait_send()


def finish(size, lm, mm, coef, eddy_out, lm_out, mm_out, coef_out, eddy, sem):
    copies = [
        pltpu.make_async_copy(lm, lm_out, sem.at[0]),
        pltpu.make_async_copy(mm, mm_out, sem.at[1]),
        pltpu.make_async_copy(coef.at[0], coef_out, sem.at[2]),
        pltpu.make_async_copy(eddy, eddy_out, sem.at[3]),
    ]
    for copy in copies[:3]:
        copy.start()
    eddy[...] = size[...] * coef[1:2, :].reshape(1, 1, coef.shape[1])
    copies[3].start()
    for copy in copies:
        copy.wait()


def solution(mesh):
    shape = (8, 2, 4, 2, 2)
    torus = Mesh(mesh.devices.reshape(shape), AXES)

    def per_device(velocity, y_gap):
        _, nx, depth, height = velocity.shape
        chunks, tiles = height // LANES, depth // ROWS
        cells = nx * lax.axis_size(GX) * depth * lax.axis_size(GZ)
        rims = 2 + 2 * tiles + 4
        ways = shape[1] * shape[3] * shape[4] + shape[2] + shape[0]
        grid = jax.ShapeDtypeStruct((nx, depth, height), jnp.float32)
        vmem = pl.BlockSpec(memory_space=pltpu.VMEM)
        hbm = pl.BlockSpec(memory_space=pltpu.HBM)
        size, lm, mm, coefficient = pl.pallas_call(
            lambda *refs: kernel(shape, cells, *refs),
            out_shape=(grid, grid, grid, jax.ShapeDtypeStruct((2, height), jnp.float32)),
            in_specs=[hbm, hbm],
            out_specs=(vmem, vmem, vmem, vmem),
            scratch_shapes=[
                pltpu.VMEM((3, chunks, nx + 4, depth + 16, LANES), jnp.float32),
                pltpu.VMEM((22, chunks, nx + 2, depth + 8, LANES), jnp.float32),
                pltpu.VMEM((height,), jnp.float32),
                pltpu.SMEM((height + 1,), jnp.float32),
                pltpu.VMEM((4, height), jnp.float32),
                pltpu.VMEM((2 * chunks, ROWS, LANES), jnp.float32),
                pltpu.VMEM((3, ROWS, LANES), jnp.float32),
                pltpu.VMEM((ways, ROWS, LANES), jnp.float32),
                pltpu.SemaphoreType.DMA((3 * chunks + 2,)),
                pltpu.SemaphoreType.DMA((rims,)),
                pltpu.SemaphoreType.DMA((rims,)),
                pltpu.SemaphoreType.DMA((ways,)),
                pltpu.SemaphoreType.DMA((ways,)),
            ],
            compiler_params=pltpu.CompilerParams(
                collective_id=0, has_side_effects=True, vmem_limit_bytes=40 * 1024 * 1024
            ),
            name="smagorinsky",
        )(pltpu.with_memory_space_constraint(velocity, pltpu.HBM), pltpu.with_memory_space_constraint(y_gap, pltpu.HBM))
        return pl.pallas_call(
            finish,
            out_shape=(grid, grid, grid, jax.ShapeDtypeStruct((height,), jnp.float32)),
            in_specs=[vmem] * 4,
            out_specs=[hbm] * 4,
            scratch_shapes=[pltpu.VMEM((nx, depth, height), jnp.float32), pltpu.SemaphoreType.DMA((4,))],
            compiler_params=pltpu.CompilerParams(vmem_limit_bytes=4 * 1024 * 1024),
            name="finish",
        )(size, lm, mm, coefficient)

    return jax.shard_map(
        per_device,
        mesh=torus,
        in_specs=(P(None, GX, GZ, None), P()),
        out_specs=(P(GX, GZ, None), P(GX, GZ, None), P(GX, GZ, None), P()),
        check_vma=False,
    )
```

time: 48 us -> 41.2 us (0.86)
  local copies, waits for them, and re-layouts: 3.51 us -> 0 us
  Pallas kernels: 42.2 us -> 40.5 us
  other arithmetic: 1.47 us -> 0 us
    unnamed x5 -> x0, local copies, waits for them, and re-layouts: 3.5 us -> none
    pallas_call x1, Pallas kernels: 42.2 us -> 39.5 us  [per_device(): pl.pallas_call(lambda *refs: kernel(shape, cells, *refs), out_shape=(grid...]
    pallas_call x0 -> x1, Pallas kernels: none -> 1.05 us  [per_device(): pl.pallas_call(finish, out_shape=(grid, grid, grid, jax.ShapeDtypeStruct(...]
    mul x2 -> x0, other arithmetic: 0.86 us -> none  [the longest x1 0.85 us: per_device(): width_sq * (1.0 / 256.0)]
    pallas_call x1 -> x0, other arithmetic: 0.6 us -> none  [per_device(): pl.pallas_call(lambda *refs: kernel(shape, cells, *refs), out_shape=(grid...]
where the time goes in v2:
time: 41.2 us; the launch traced here: 41.1 us
  Pallas kernels  40.5 us (98%)
  between operations  0.64 us (2%)
    pallas_call x1, Pallas kernels, per_device(): pl.pallas_call(lambda *refs: kernel(shape, cells, *refs), out_shape=(grid...  39.5 us
    pallas_call x1, Pallas kernels, per_device(): pl.pallas_call(finish, out_shape=(grid, grid, grid, jax.ShapeDtypeStruct(...  1.05 us

profile of v2, /device:TPU:1, one launch (start us, length us, event | category | flops | bytes accessed | tf_op | source)
XLA Modules:
  0.0 41.1 jit_solution(11508617028341290664)
XLA Ops:
  0.6 39.5 %smagorinsky.1 = (f32[8,32,384]{2,1,0:T(8,128)S(1)}, f32[8,32,384]{2,1,0:T(8,128)S(1)}, f32[8,32,384]{2,1,0:T(8,128)S(1)}, f32[2,384]{1,0:T(2,128)S(1)}) custom-call(f32[3,8,32,384]{3,2,1,0:T(8,128)} %refs_0_.1, f32[385]{0:T(512)} %refs_1_.1), custom_call_target="tpu_custom_call" | custom-call | tf_op jit(solution)/shard_map/smagorinsky/pallas_call | solution.py:316
  40.1 1.0 %finish.1 = (f32[8,32,384]{2,1,0:T(8,128)}, f32[8,32,384]{2,1,0:T(8,128)}, f32[8,32,384]{2,1,0:T(8,128)}, f32[384]{0:T(512)}) custom-call(f32[8,32,384]{2,1,0:T(8,128)S(1)} %get-tuple-element.8.size, f32[8,32,384]{2,1,0:T(8,128)S(1)} %get-tuple-element.9.lm, f32[8,32,384]{2,1,0:T(8,128)S(1)} %get-tuple-element.10.mm, f32[2,384]{1,0:T(2,128)S(1)} %get-tuple-element.11.coef), custom_call_target="tpu_custom_call" | custom-call | tf_op jit(solution)/shard_map/finish/pallas_call | solution.py:341

commit v3 on v2

--- a/solution.py
+++ b/solution.py
@@ -1,3 +1,6 @@
+import itertools
+import math
+
 import jax
 import jax.numpy as jnp
 from jax import lax
@@ -13,6 +16,10 @@
 
 LANES = 128
 ROWS = 8
+STAGES = ((4,), (1, 2, 3), (0,))
+OFFSET = 8
+AHEAD = 6
+CUTS = (0, 11, 19, 27)
 TINY = 1.1754944e-38
 
 
@@ -34,12 +41,14 @@
             loads.append(
                 pltpu.make_async_copy(
                     vel.at[part, :, :, pl.ds(chunk * LANES, LANES)],
-                    pad.at[part, chunk, pl.ds(2, nx), pl.ds(2, depth), :],
+                    pad.at[part, chunk, pl.ds(2, nx), pl.ds(OFFSET, depth), :],
                     load_sem.at[part * chunks + chunk],
                 )
             )
     loads.append(pltpu.make_async_copy(y_gap.at[pl.ds(0, chunks * LANES)], gap, load_sem.at[3 * chunks]))
     loads.append(pltpu.make_async_copy(y_gap, last, load_sem.at[3 * chunks + 1]))
+    for load in loads:
+        load.start()
 
     def along_x(step):
         ring = nz * nxl
@@ -55,30 +64,25 @@
         z, xl, *_ = along_x(gx_step)
         return (z, xl, *along_z(gz_step)[2:])
 
-    def near(off, sign):
-        xl, xh, c = (lax.rem(m + sign * o + n, n) for m, o, n in zip((me[1], me[3], me[4]), off, (nxl, nxh, nc)))
-        return (me[0], xl, me[2], xh, c)
-
-    def on_y(off, sign):
-        return (me[0], me[1], lax.rem(me[2] + sign * off + ny, ny), me[3], me[4])
-
-    def on_z(off, sign):
-        return (lax.rem(me[0] + sign * off + nz, nz), *me[1:])
-
-    group = [(a, b, c) for a in range(nxl) for b in range(nxh) for c in range(nc)]
-    stages = (
-        (near, group[1:], lambda spot: (spot[1] * nxh + spot[3]) * nc + spot[4], len(group)),
-        (on_y, range(1, ny), lambda spot: spot[2], ny),
-        (on_z, range(1, nz), lambda spot: spot[0], nz),
-    )
+    def shifted(axes, off, sign):
+        spot = list(me)
+        for axis, step in zip(axes, off):
+            spot[axis] = lax.rem(me[axis] + sign * step + sizes[axis], sizes[axis])
+        return tuple(spot)
+
+    def slot_of(axes, spot):
+        slot = 0
+        for axis in axes:
+            slot = slot * sizes[axis] + spot[axis]
+        return slot
+
+    stages = [(axes, list(itertools.product(*(range(sizes[axis]) for axis in axes)))) for axes in STAGES]
 
     barrier = pltpu.get_barrier_semaphore()
     steps = [(1, 0), (-1, 0), (0, 1), (0, -1), (1, 1), (1, -1), (-1, 1), (-1, -1)]
-    greeted = [around(*step) for step in steps] + [to(off, 1) for to, offs, _, _ in stages for off in offs]
+    greeted = [around(*step) for step in steps] + [shifted(axes, off, 1) for axes, offs in stages for off in offs[1:]]
     for other in greeted:
         pl.semaphore_signal(barrier, inc=1, device_id=other, device_id_type=MESH)
-    for load in loads:
-        load.start()
     acc[...] = jnp.zeros_like(acc)
     for load in loads:
         load.wait()
@@ -96,26 +100,28 @@
 
     up, down, right, left = along_x(1), along_x(-1), along_z(1), along_z(-1)
     body = (2, nx)
+    first_two, last_two = (OFFSET, 2), (OFFSET + depth - 2, 2)
+    before, behind = (OFFSET - 2, 2), (OFFSET + depth, 2)
     sides = [
-        rim(0, (body, (depth, 2)), (body, (0, 2)), right),
-        rim(1, (body, (2, 2)), (body, (depth + 2, 2)), left),
+        rim(0, (body, last_two), (body, before), right),
+        rim(1, (body, first_two), (body, behind), left),
     ]
     strips = []
-    for tile in range(tiles):
-        cut = (2 + ROWS * tile, ROWS)
+    cuts = [(OFFSET + a, b - a) for a, b in zip(CUTS, CUTS[1:] + (depth,))]
+    for number, cut in enumerate(cuts):
         strips.append((
-            rim(2 + 2 * tile, ((nx, 2), cut), ((0, 2), cut), up),
-            rim(3 + 2 * tile, ((2, 2), cut), ((nx + 2, 2), cut), down),
+            rim(2 + 2 * number, ((nx, 2), cut), ((0, 2), cut), up),
+            rim(3 + 2 * number, ((2, 2), cut), ((nx + 2, 2), cut), down),
         ))
-    first = 2 + 2 * tiles
+    first = 2 + 2 * len(cuts)
     corners = [
-        rim(first, ((nx, 2), (depth, 2)), ((0, 2), (0, 2)), around(1, 1)),
-        rim(first + 1, ((nx, 2), (2, 2)), ((0, 2), (depth + 2, 2)), around(1, -1)),
-        rim(first + 2, ((2, 2), (depth, 2)), ((nx + 2, 2), (0, 2)), around(-1, 1)),
-        rim(first + 3, ((2, 2), (2, 2)), ((nx + 2, 2), (depth + 2, 2)), around(-1, -1)),
+        rim(first, ((nx, 2), last_two), ((0, 2), before), around(1, 1)),
+        rim(first + 1, ((nx, 2), first_two), ((0, 2), behind), around(1, -1)),
+        rim(first + 2, ((2, 2), last_two), ((nx + 2, 2), before), around(-1, 1)),
+        rim(first + 3, ((2, 2), first_two), ((nx + 2, 2), behind), around(-1, -1)),
     ]
 
-    for copy in sides + corners + [strip for pair in strips for strip in pair]:
+    for copy in sides + corners:
         copy.start()
 
     lane = lax.broadcasted_iota(jnp.int32, (ROWS, LANES), 1)
@@ -137,7 +143,7 @@
         gaps[3:4, line] = width_sq
 
     def strains(row, tile):
-        here, at = row + 2, ROWS * tile + 1
+        here, at = row + 2, ROWS * tile - AHEAD + OFFSET
 
         def speed(part, chunk, dx=0, dz=0):
             return pad[part, chunk, here + dx, pl.ds(at + dz, ROWS), :]
@@ -181,7 +187,7 @@
             def smooth(number):
                 lines = []
                 for k in range(4):
-                    a, b, c = (field[number, chunk, row + k, pl.ds(ROWS * tile + dz, ROWS), :] for dz in range(3))
+                    a, b, c = (field[number, chunk, row + k, pl.ds(ROWS * tile + AHEAD + dz, ROWS), :] for dz in (-1, 0, 1))
                     lines.append((a + c) + (b + b))
                 pair = [lines[k] + lines[k + 1] for k in range(3)]
                 return [pair[k] + pair[k + 1] for k in range(2)]
@@ -208,7 +214,7 @@
             mm = [mm_scale * (a + 0.5 * b) for a, b in zip(mm_d, mm_o)]
             for k in range(2):
                 spot = (row + k, pl.ds(ROWS * tile, ROWS), pl.ds(chunk * LANES, LANES))
-                size_out[spot] = field[21, chunk, row + k + 1, pl.ds(ROWS * tile + 1, ROWS), :]
+                size_out[spot] = field[21, chunk, row + k + 1, pl.ds(ROWS * tile + AHEAD, ROWS), :]
                 lm_out[spot] = lm[k]
                 mm_out[spot] = mm[k]
             acc[chunk] += lm[0] + lm[1]
@@ -220,24 +226,36 @@
             return carry
         lax.fori_loop(0, (stop - start) // step, turn, 0)
 
-    for tile in range(1, tiles - 1):
+    over(1, nx - 1, lambda row: strains(row, 1))
+    for side in sides:
+        side.wait_send()
+    for pair in strips:
+        for strip in pair:
+            strip.start()
+    for tile in range(2, tiles):
         over(1, nx - 1, lambda row, tile=tile: strains(row, tile))
     for side in sides:
         side.wait_recv()
-    for tile in (0, tiles - 1, tiles):
+    for tile in (0, tiles):
         over(1, nx - 1, lambda row, tile=tile: strains(row, tile))
     for tile in range(tiles):
         over(2, nx - 2, lambda row, tile=tile: model(row, tile), step=2)
 
-    edges = ((-1, 0, 0), (nx - 1, nx - 1, nx - 2))
-    for tile in range(tiles + 1):
-        for side, (start, _, block) in enumerate(edges):
-            if tile == 0:
-                corners[2 * side].wait_recv()
-                corners[2 * side + 1].wait_recv()
-            if tile < tiles:
-                strips[tile][side].wait_recv()
-            over(start, start + 2, lambda row, tile=tile: strains(row, tile))
+    for turn in range(2):
+        side = me[1] if turn == 0 else 1 - me[1]
+        rows, start, block = side * (nx + 2), side * nx - 1, side * (nx - 2)
+
+        def landed(number, cut):
+            there = pad.at[:, :, pl.ds(rows, 2), pl.ds(*cut), :]
+            pltpu.make_async_copy(there, there, recv_sem.at[number]).wait()
+
+        landed(first + 2 * side, before)
+        for tile in range(tiles + 1):
+            if tile != 1:
+                landed(2 + 2 * max(tile - 1, 0) + side, cuts[max(tile - 1, 0)])
+            if tile == tiles:
+                landed(first + 1 + 2 * side, behind)
+            over(0, 2, lambda row, tile=tile: strains(start + row, tile))
             if tile:
                 model(block, tile - 1)
 
@@ -246,33 +264,26 @@
     for number in range(2 * chunks, ROWS):
         sent[0, number : number + 1, :] = jnp.zeros((1, LANES), jnp.float32)
     total = sent[0]
-    copies, base = [], 0
-    for number, (to, offs, slot_of, count) in enumerate(stages):
+    held, messages, base = 2 * chunks, 0, 0
+    for number, (axes, offs) in enumerate(stages):
         if number:
             sent[number] = total
-        mine = base + slot_of(me)
+        mine = base + slot_of(axes, me)
+        for off in offs[1:]:
+            pltpu.make_async_remote_copy(
+                src_ref=sent.at[number, pl.ds(0, held)], dst_ref=got.at[mine, pl.ds(0, held)],
+                send_sem=sum_send.at[0], recv_sem=sum_recv.at[number],
+                device_id=shifted(axes, off, 1), device_id_type=MESH,
+            ).start()
         got[mine] = total
-        for off in offs:
-            copy = pltpu.make_async_remote_copy(
-                src_ref=sent.at[number], dst_ref=got.at[mine],
-                send_sem=sum_send.at[len(copies)], recv_sem=sum_recv.at[mine],
-                device_id=to(off, 1), device_id_type=MESH,
-            )
-            copy.start()
-            copies.append(copy)
-        for off in offs:
-            other = to(off, -1)
-            slot = base + slot_of(other)
-            pltpu.make_async_remote_copy(
-                src_ref=sent.at[number], dst_ref=got.at[slot],
-                send_sem=sum_send.at[0], recv_sem=sum_recv.at[slot],
-                device_id=other, device_id_type=MESH,
-            ).wait_recv()
-        terms = [got[base + k] for k in range(count)]
+        others = got.at[pl.ds(base, len(offs) - 1), pl.ds(0, held)]
+        pltpu.make_async_copy(others, others, sum_recv.at[number]).wait()
+        terms = [got[base + k] for k in range(len(offs))]
         while len(terms) > 1:
             terms = [a + b for a, b in zip(terms[::2], terms[1::2])]
         total = terms[0]
-        base += count
+        base += len(offs)
+        messages += len(offs) - 1
 
     for chunk in range(chunks):
         line = pl.ds(chunk * LANES, LANES)
@@ -281,8 +292,10 @@
         coefficient = share / below
         coef_out[0:1, line] = coefficient
         coef_out[1:2, line] = coefficient * gaps[3:4, line]
-    for copy in sides + corners + [strip for pair in strips for strip in pair] + copies:
+    for copy in corners + [strip for pair in strips for strip in pair]:
         copy.wait_send()
+    others = got.at[pl.ds(0, messages), pl.ds(0, held)]
+    pltpu.make_async_copy(others, others, sum_send.at[0]).wait()
 
 
 def finish(size, lm, mm, coef, eddy_out, lm_out, mm_out, coef_out, eddy, sem):
@@ -308,8 +321,8 @@
         _, nx, depth, height = velocity.shape
         chunks, tiles = height // LANES, depth // ROWS
         cells = nx * lax.axis_size(GX) * depth * lax.axis_size(GZ)
-        rims = 2 + 2 * tiles + 4
-        ways = shape[1] * shape[3] * shape[4] + shape[2] + shape[0]
+        rims = 2 + 2 * len(CUTS) + 4
+        ways = sum(math.prod(shape[axis] for axis in axes) for axes in STAGES)
         grid = jax.ShapeDtypeStruct((nx, depth, height), jnp.float32)
         vmem = pl.BlockSpec(memory_space=pltpu.VMEM)
         hbm = pl.BlockSpec(memory_space=pltpu.HBM)
@@ -325,13 +338,13 @@
                 pltpu.SMEM((height + 1,), jnp.float32),
                 pltpu.VMEM((4, height), jnp.float32),
                 pltpu.VMEM((2 * chunks, ROWS, LANES), jnp.float32),
-                pltpu.VMEM((3, ROWS, LANES), jnp.float32),
+                pltpu.VMEM((len(STAGES), ROWS, LANES), jnp.float32),
                 pltpu.VMEM((ways, ROWS, LANES), jnp.float32),
                 pltpu.SemaphoreType.DMA((3 * chunks + 2,)),
                 pltpu.SemaphoreType.DMA((rims,)),
                 pltpu.SemaphoreType.DMA((rims,)),
-                pltpu.SemaphoreType.DMA((ways,)),
-                pltpu.SemaphoreType.DMA((ways,)),
+                pltpu.SemaphoreType.DMA((1,)),
+                pltpu.SemaphoreType.DMA((len(STAGES),)),
             ],
             compiler_params=pltpu.CompilerParams(
                 collective_id=0, has_side_effects=True, vmem_limit_bytes=40 * 1024 * 1024

time: 41.2 us -> 39.9 us (0.968); the launches traced: 41.1 us -> 39.1 us
  Pallas kernels: 40.5 us -> 38.5 us
    pallas_call x1, Pallas kernels: 39.5 us -> 37.5 us  [per_device(): pl.pallas_call(lambda *refs: kernel(shape, cells, *refs), out_shape=(grid...]
where the time goes in v3:
time: 39.9 us; the launch traced here: 39.1 us
  Pallas kernels  38.5 us (96%)
  between operations  0.64 us (2%)
    pallas_call x1, Pallas kernels, per_device(): pl.pallas_call(lambda *refs: kernel(shape, cells, *refs), out_shape=(grid...  37.5 us
    pallas_call x1, Pallas kernels, per_device(): pl.pallas_call(finish, out_shape=(grid, grid, grid, jax.ShapeDtypeStruct(...  1.05 us

profile of v3, /device:TPU:1, one launch (start us, length us, event | category | flops | bytes accessed | tf_op | source)
XLA Modules:
  0.0 39.1 jit_solution(12447461977095602891)
XLA Ops:
  0.6 37.5 %smagorinsky.1 = (f32[8,32,384]{2,1,0:T(8,128)S(1)}, f32[8,32,384]{2,1,0:T(8,128)S(1)}, f32[8,32,384]{2,1,0:T(8,128)S(1)}, f32[2,384]{1,0:T(2,128)S(1)}) custom-call(f32[3,8,32,384]{3,2,1,0:T(8,128)} %refs_0_.1, f32[385]{0:T(512)} %refs_1_.1), custom_call_target="tpu_custom_call" | custom-call | tf_op jit(solution)/shard_map/smagorinsky/pallas_call | solution.py:329
  38.1 1.0 %finish.1 = (f32[8,32,384]{2,1,0:T(8,128)}, f32[8,32,384]{2,1,0:T(8,128)}, f32[8,32,384]{2,1,0:T(8,128)}, f32[384]{0:T(512)}) custom-call(f32[8,32,384]{2,1,0:T(8,128)S(1)} %get-tuple-element.8.size, f32[8,32,384]{2,1,0:T(8,128)S(1)} %get-tuple-element.9.lm, f32[8,32,384]{2,1,0:T(8,128)S(1)} %get-tuple-element.10.mm, f32[2,384]{1,0:T(2,128)S(1)} %get-tuple-element.11.coef), custom_call_target="tpu_custom_call" | custom-call | tf_op jit(solution)/shard_map/finish/pallas_call | solution.py:354

commit v4 on v3

--- a/solution.py
+++ b/solution.py
@@ -1,5 +1,4 @@
 import itertools
-import math
 
 import jax
 import jax.numpy as jnp
@@ -16,7 +15,6 @@
 
 LANES = 128
 ROWS = 8
-STAGES = ((4,), (1, 2, 3), (0,))
 OFFSET = 8
 AHEAD = 6
 CUTS = (0, 11, 19, 27)
@@ -64,29 +62,39 @@
         z, xl, *_ = along_x(gx_step)
         return (z, xl, *along_z(gz_step)[2:])
 
-    def shifted(axes, off, sign):
+    outer = me[4] == nc - 1
+
+    def shifted(axes, off, sign=1):
         spot = list(me)
         for axis, step in zip(axes, off):
             spot[axis] = lax.rem(me[axis] + sign * step + sizes[axis], sizes[axis])
         return tuple(spot)
 
-    def slot_of(axes, spot):
-        slot = 0
-        for axis in axes:
-            slot = slot * sizes[axis] + spot[axis]
-        return slot
-
-    stages = [(axes, list(itertools.product(*(range(sizes[axis]) for axis in axes)))) for axes in STAGES]
+    in_plane, in_line = (1, 2, 3), (0, 4)
+    plane_offs = list(itertools.product(range(nxl), range(ny), range(nxh)))[1:]
+    line_offs = [(step, 0) for step in range(1, nz)] + [(step, 1) for step in range(nz)]
+    plane_mine = (me[1] * ny + me[2]) * nxh + me[3]
+    members = len(plane_offs) + 1
 
     barrier = pltpu.get_barrier_semaphore()
     steps = [(1, 0), (-1, 0), (0, 1), (0, -1), (1, 1), (1, -1), (-1, 1), (-1, -1)]
-    greeted = [around(*step) for step in steps] + [shifted(axes, off, 1) for axes, offs in stages for off in offs[1:]]
+    greeted = [around(*step) for step in steps] + [shifted(in_line, off) for off in line_offs]
     for other in greeted:
         pl.semaphore_signal(barrier, inc=1, device_id=other, device_id_type=MESH)
+
+    for off in plane_offs:
+        there = shifted(in_plane, off)
+        pl.semaphore_signal(barrier, inc=1, device_id=(*there[:4], 1 - me[4]), device_id_type=MESH)
+
+    @pl.when(outer)
+    def _():
+        for off in plane_offs:
+            pl.semaphore_signal(barrier, inc=1, device_id=shifted(in_plane, off), device_id_type=MESH)
+
     acc[...] = jnp.zeros_like(acc)
     for load in loads:
         load.wait()
-    pl.semaphore_wait(barrier, len(greeted))
+    pl.semaphore_wait(barrier, len(greeted) + jnp.where(outer, 2, 1) * len(plane_offs))
 
     def rim(number, source, target, other):
         return pltpu.make_async_remote_copy(
@@ -121,7 +129,7 @@
         rim(first + 3, ((2, 2), first_two), ((nx + 2, 2), behind), around(-1, -1)),
     ]
 
-    for copy in sides + corners:
+    for copy in sides + corners + [strip for pair in strips for strip in pair]:
         copy.start()
 
     lane = lax.broadcasted_iota(jnp.int32, (ROWS, LANES), 1)
@@ -143,51 +151,55 @@
         gaps[3:4, line] = width_sq
 
     def strains(row, tile):
-        here, at = row + 2, ROWS * tile - AHEAD + OFFSET
-
-        def speed(part, chunk, dx=0, dz=0):
-            return pad[part, chunk, here + dx, pl.ds(at + dz, ROWS), :]
-
-        middle = [[speed(part, chunk) for chunk in range(chunks)] for part in range(3)]
-        before = [[pltpu.roll(v, 1, 1) for v in parts] for parts in middle]
-        after = [[pltpu.roll(v, LANES - 1, 1) for v in parts] for parts in middle]
-        for chunk in range(chunks):
-            rate = jnp.broadcast_to(gaps[0:1, pl.ds(chunk * LANES, LANES)], (ROWS, LANES))
-
-            def slope_y(part):
-                upper = jnp.where(high, after[part][chunk + 1] if chunk + 1 < chunks else zero, after[part][chunk])
-                lower = jnp.where(low, before[part][chunk - 1] if chunk else zero, before[part][chunk])
-                return (upper - lower) * rate
-
-            def slope_x(part):
-                return speed(part, chunk, dx=1) - speed(part, chunk, dx=-1)
-
-            def slope_z(part):
-                return speed(part, chunk, dz=1) - speed(part, chunk, dz=-1)
-
-            strain = [
-                slope_x(0),
-                slope_y(1),
-                slope_z(2),
-                slope_y(0) + slope_x(1),
-                slope_z(0) + slope_x(2),
-                slope_z(1) + slope_y(2),
-            ]
-            ours = [middle[part][chunk] for part in range(3)]
-            square = [s * s for s in strain]
-            size = root(0.5 * (square[0] + square[1] + square[2]) + 0.25 * (square[3] + square[4] + square[5]))
-            pairs = [ours[0] * ours[0], ours[1] * ours[1], ours[2] * ours[2],
-                     ours[0] * ours[1], ours[0] * ours[2], ours[1] * ours[2]]
-            values = strain + [size * s for s in strain] + pairs + ours + [size]
-            for number, value in enumerate(values):
-                field[number, chunk, row + 1, pl.ds(ROWS * tile, ROWS), :] = value
+        at = pl.multiple_of(ROWS * tile, ROWS) + (OFFSET - AHEAD)
+
+        def speed(line, part, chunk, dx=0, dz=0):
+            return pad[part, chunk, row + line + 2 + dx, pl.ds(at + dz, ROWS), :]
+
+        lines, parts = range(2), range(3)
+        middle = [[[speed(line, part, chunk) for chunk in range(chunks)] for part in parts] for line in lines]
+        before = [[[pltpu.roll(v, 1, 1) for v in vs] for vs in rows] for rows in middle]
+        after = [[[pltpu.roll(v, LANES - 1, 1) for v in vs] for vs in rows] for rows in middle]
+        for line in lines:
+            for chunk in range(chunks):
+                rate = jnp.broadcast_to(gaps[0:1, pl.ds(chunk * LANES, LANES)], (ROWS, LANES))
+
+                def slope_y(part):
+                    above, below = after[line][part], before[line][part]
+                    upper = jnp.where(high, above[chunk + 1] if chunk + 1 < chunks else zero, above[chunk])
+                    lower = jnp.where(low, below[chunk - 1] if chunk else zero, below[chunk])
+                    return (upper - lower) * rate
+
+                def slope_x(part):
+                    return speed(line, part, chunk, dx=1) - speed(line, part, chunk, dx=-1)
+
+                def slope_z(part):
+                    return speed(line, part, chunk, dz=1) - speed(line, part, chunk, dz=-1)
+
+                strain = [
+                    slope_x(0),
+                    slope_y(1),
+                    slope_z(2),
+                    slope_y(0) + slope_x(1),
+                    slope_z(0) + slope_x(2),
+                    slope_z(1) + slope_y(2),
+                ]
+                ours = [middle[line][part][chunk] for part in parts]
+                square = [s * s for s in strain]
+                size = root(0.5 * (square[0] + square[1] + square[2]) + 0.25 * (square[3] + square[4] + square[5]))
+                pairs = [ours[0] * ours[0], ours[1] * ours[1], ours[2] * ours[2],
+                         ours[0] * ours[1], ours[0] * ours[2], ours[1] * ours[2]]
+                values = strain + [size * s for s in strain] + pairs + ours + [size]
+                for number, value in enumerate(values):
+                    field[number, chunk, row + line + 1, pl.ds(pl.multiple_of(ROWS * tile, ROWS), ROWS), :] = value
 
     def model(row, tile):
+        base = pl.multiple_of(ROWS * tile, ROWS)
         for chunk in range(chunks):
             def smooth(number):
                 lines = []
                 for k in range(4):
-                    a, b, c = (field[number, chunk, row + k, pl.ds(ROWS * tile + AHEAD + dz, ROWS), :] for dz in (-1, 0, 1))
+                    a, b, c = (field[number, chunk, row + k, pl.ds(base + AHEAD + dz, ROWS), :] for dz in (-1, 0, 1))
                     lines.append((a + c) + (b + b))
                 pair = [lines[k] + lines[k + 1] for k in range(3)]
                 return [pair[k] + pair[k + 1] for k in range(2)]
@@ -213,77 +225,115 @@
             lm = [lm_scale * v for v in lm]
             mm = [mm_scale * (a + 0.5 * b) for a, b in zip(mm_d, mm_o)]
             for k in range(2):
-                spot = (row + k, pl.ds(ROWS * tile, ROWS), pl.ds(chunk * LANES, LANES))
-                size_out[spot] = field[21, chunk, row + k + 1, pl.ds(ROWS * tile + AHEAD, ROWS), :]
+                spot = (row + k, pl.ds(base, ROWS), pl.ds(chunk * LANES, LANES))
+                size_out[spot] = field[21, chunk, row + k + 1, pl.ds(base + AHEAD, ROWS), :]
                 lm_out[spot] = lm[k]
                 mm_out[spot] = mm[k]
             acc[chunk] += lm[0] + lm[1]
             acc[chunks + chunk] += mm[0] + mm[1]
 
-    def over(start, stop, call, step=1):
-        def turn(k, carry):
-            call(start + step * k)
+    inner, models = tiles, 2 * tiles - 2
+    joint = models + tiles
+
+    def step(k, carry):
+        second = k > joint + 1
+        side = jnp.where(second, 1 - me[1], me[1])
+        edge = jnp.logical_and(k >= models, k != joint)
+        spot = jnp.where(second, k - joint - 2, jnp.where(k > joint, tiles, k - models))
+
+        @pl.when(k == inner - 1)
+        def _():
+            sides[0].wait_recv()
+
+        @pl.when(k == joint)
+        def _():
+            sides[1].wait_recv()
+
+        def landed(number, cut):
+            there = pad.at[:, :, pl.ds(side * (nx + 2), 2), pl.ds(*cut), :]
+            pltpu.make_async_copy(there, there, recv_sem.at[number]).wait()
+
+        for number, cut in enumerate(cuts):
+            @pl.when(jnp.logical_and(edge, spot == (number + 1 if number else 0)))
+            def _(number=number, cut=cut):
+                if number == 0:
+                    landed(first + 2 * side, before)
+                landed(2 + 2 * number + side, cut)
+                if number == len(cuts) - 1:
+                    landed(first + 1 + 2 * side, behind)
+
+        tile = jnp.where(edge, spot, jnp.where(k == joint, tiles, jnp.where(k == inner - 1, 0, k + 1)))
+        start = jnp.where(edge, side * nx - 1, 1)
+        count = jnp.where(edge, 1, jnp.where(jnp.logical_or(k < inner, k == joint), (nx - 2) // 2, 0))
+
+        def strain_turn(row, carry):
+            strains(start + 2 * row, tile)
             return carry
-        lax.fori_loop(0, (stop - start) // step, turn, 0)
-
-    over(1, nx - 1, lambda row: strains(row, 1))
-    for side in sides:
-        side.wait_send()
-    for pair in strips:
-        for strip in pair:
-            strip.start()
-    for tile in range(2, tiles):
-        over(1, nx - 1, lambda row, tile=tile: strains(row, tile))
-    for side in sides:
-        side.wait_recv()
-    for tile in (0, tiles):
-        over(1, nx - 1, lambda row, tile=tile: strains(row, tile))
-    for tile in range(tiles):
-        over(2, nx - 2, lambda row, tile=tile: model(row, tile), step=2)
-
-    for turn in range(2):
-        side = me[1] if turn == 0 else 1 - me[1]
-        rows, start, block = side * (nx + 2), side * nx - 1, side * (nx - 2)
-
-        def landed(number, cut):
-            there = pad.at[:, :, pl.ds(rows, 2), pl.ds(*cut), :]
-            pltpu.make_async_copy(there, there, recv_sem.at[number]).wait()
-
-        landed(first + 2 * side, before)
-        for tile in range(tiles + 1):
-            if tile != 1:
-                landed(2 + 2 * max(tile - 1, 0) + side, cuts[max(tile - 1, 0)])
-            if tile == tiles:
-                landed(first + 1 + 2 * side, behind)
-            over(0, 2, lambda row, tile=tile: strains(start + row, tile))
-            if tile:
-                model(block, tile - 1)
+        lax.fori_loop(0, count, strain_turn, 0)
+
+        model_tile = jnp.where(edge, spot - 1, jnp.where(k == joint, tiles - 1, k - inner + 1))
+        block = jnp.where(edge, side * (nx - 2), 2)
+        turns = jnp.where(edge, jnp.where(spot > 0, 1, 0), jnp.where(k < inner - 1, 0, (nx - 4) // 2))
+
+        def model_turn(turn, carry):
+            model(block + 2 * turn, model_tile)
+            return carry
+        lax.fori_loop(0, turns, model_turn, 0)
+        return carry
+
+    lax.fori_loop(0, joint + tiles + 3, step, 0)
 
     for number in range(2 * chunks):
         sent[0, number : number + 1, :] = jnp.sum(acc[number], axis=0, keepdims=True)
     for number in range(2 * chunks, ROWS):
         sent[0, number : number + 1, :] = jnp.zeros((1, LANES), jnp.float32)
-    total = sent[0]
-    held, messages, base = 2 * chunks, 0, 0
-    for number, (axes, offs) in enumerate(stages):
-        if number:
-            sent[number] = total
-        mine = base + slot_of(axes, me)
-        for off in offs[1:]:
-            pltpu.make_async_remote_copy(
-                src_ref=sent.at[number, pl.ds(0, held)], dst_ref=got.at[mine, pl.ds(0, held)],
-                send_sem=sum_send.at[0], recv_sem=sum_recv.at[number],
-                device_id=shifted(axes, off, 1), device_id_type=MESH,
-            ).start()
-        got[mine] = total
-        others = got.at[pl.ds(base, len(offs) - 1), pl.ds(0, held)]
-        pltpu.make_async_copy(others, others, sum_recv.at[number]).wait()
-        terms = [got[base + k] for k in range(len(offs))]
+    held = 2 * chunks
+
+    def send(source, slot, number, other):
+        pltpu.make_async_remote_copy(
+            src_ref=sent.at[source, pl.ds(0, held)], dst_ref=got.at[slot, pl.ds(0, held)],
+            send_sem=sum_send.at[0], recv_sem=sum_recv.at[number],
+            device_id=other, device_id_type=MESH,
+        ).start()
+
+    def arrived(start, count, sem):
+        there = got.at[pl.ds(start, count), pl.ds(0, held)]
+        pltpu.make_async_copy(there, there, sem).wait()
+
+    def added(terms):
         while len(terms) > 1:
             terms = [a + b for a, b in zip(terms[::2], terms[1::2])]
-        total = terms[0]
-        base += len(offs)
-        messages += len(offs) - 1
+        return terms[0]
+
+    line_at = 2 * members
+
+    def to_outer(off):
+        spot = shifted(in_plane, off)
+        return (*spot[:4], nc - 1)
+
+    @pl.when(jnp.logical_not(outer))
+    def _():
+        for off in [(0, 0, 0)] + plane_offs:
+            send(0, plane_mine, 1, to_outer(off))
+        arrived(0, members, sum_send.at[0])
+        arrived(line_at, nz, sum_recv.at[2])
+
+    @pl.when(outer)
+    def _():
+        for off in plane_offs:
+            send(0, members + plane_mine, 1, shifted(in_plane, off))
+        got[members + plane_mine] = sent[0]
+        arrived(0, 2 * members - 1, sum_recv.at[1])
+        whole = added([got[k] for k in range(2 * members)])
+        sent[1] = whole
+        for off in line_offs:
+            send(1, line_at + me[0], 2, shifted(in_line, off))
+        got[line_at + me[0]] = whole
+        arrived(line_at, nz - 1, sum_recv.at[2])
+        arrived(0, members - 1, sum_send.at[0])
+        arrived(0, len(line_offs), sum_send.at[0])
+
+    total = added([got[line_at + k] for k in range(nz)])
 
     for chunk in range(chunks):
         line = pl.ds(chunk * LANES, LANES)
@@ -292,10 +342,8 @@
         coefficient = share / below
         coef_out[0:1, line] = coefficient
         coef_out[1:2, line] = coefficient * gaps[3:4, line]
-    for copy in corners + [strip for pair in strips for strip in pair]:
+    for copy in sides + corners + [strip for pair in strips for strip in pair]:
         copy.wait_send()
-    others = got.at[pl.ds(0, messages), pl.ds(0, held)]
-    pltpu.make_async_copy(others, others, sum_send.at[0]).wait()
 
 
 def finish(size, lm, mm, coef, eddy_out, lm_out, mm_out, coef_out, eddy, sem):
@@ -322,7 +370,7 @@
         chunks, tiles = height // LANES, depth // ROWS
         cells = nx * lax.axis_size(GX) * depth * lax.axis_size(GZ)
         rims = 2 + 2 * len(CUTS) + 4
-        ways = sum(math.prod(shape[axis] for axis in axes) for axes in STAGES)
+        ways = 2 * shape[1] * shape[2] * shape[3] + shape[0]
         grid = jax.ShapeDtypeStruct((nx, depth, height), jnp.float32)
         vmem = pl.BlockSpec(memory_space=pltpu.VMEM)
         hbm = pl.BlockSpec(memory_space=pltpu.HBM)
@@ -338,13 +386,13 @@
                 pltpu.SMEM((height + 1,), jnp.float32),
                 pltpu.VMEM((4, height), jnp.float32),
                 pltpu.VMEM((2 * chunks, ROWS, LANES), jnp.float32),
-                pltpu.VMEM((len(STAGES), ROWS, LANES), jnp.float32),
+                pltpu.VMEM((2, ROWS, LANES), jnp.float32),
                 pltpu.VMEM((ways, ROWS, LANES), jnp.float32),
                 pltpu.SemaphoreType.DMA((3 * chunks + 2,)),
                 pltpu.SemaphoreType.DMA((rims,)),
                 pltpu.SemaphoreType.DMA((rims,)),
                 pltpu.SemaphoreType.DMA((1,)),
-                pltpu.SemaphoreType.DMA((len(STAGES),)),
+                pltpu.SemaphoreType.DMA((3,)),
             ],
             compiler_params=pltpu.CompilerParams(
                 collective_id=0, has_side_effects=True, vmem_limit_bytes=40 * 1024 * 1024

time: 39.9 us -> 38.7 us (0.970); the launches traced: 39.1 us -> 38.6 us
  Pallas kernels: 38.5 us -> 37.9 us
    pallas_call x1, Pallas kernels: 37.5 us -> 36.9 us  [per_device(): pl.pallas_call(lambda *refs: kernel(shape, cells, *refs), out_shape=(grid...]
where the time goes in v4:
time: 38.7 us; the launch traced here: 38.6 us
  Pallas kernels  37.9 us (98%)
  between operations  0.64 us (2%)
    pallas_call x1, Pallas kernels, per_device(): pl.pallas_call(lambda *refs: kernel(shape, cells, *refs), out_shape=(grid...  36.9 us
    pallas_call x1, Pallas kernels, per_device(): pl.pallas_call(finish, out_shape=(grid, grid, grid, jax.ShapeDtypeStruct(...  1.05 us

profile of v4, /device:TPU:1, one launch (start us, length us, event | category | flops | bytes accessed | tf_op | source)
XLA Modules:
  0.0 38.6 jit_solution(5669557690049964959)
XLA Ops:
  0.6 36.9 %smagorinsky.1 = (f32[8,32,384]{2,1,0:T(8,128)S(1)}, f32[8,32,384]{2,1,0:T(8,128)S(1)}, f32[8,32,384]{2,1,0:T(8,128)S(1)}, f32[2,384]{1,0:T(2,128)S(1)}) custom-call(f32[3,8,32,384]{3,2,1,0:T(8,128)} %refs_0_.1, f32[385]{0:T(512)} %refs_1_.1), custom_call_target="tpu_custom_call" | custom-call | tf_op jit(solution)/shard_map/smagorinsky/pallas_call | solution.py:377
  37.5 1.0 %finish.1 = (f32[8,32,384]{2,1,0:T(8,128)}, f32[8,32,384]{2,1,0:T(8,128)}, f32[8,32,384]{2,1,0:T(8,128)}, f32[384]{0:T(512)}) custom-call(f32[8,32,384]{2,1,0:T(8,128)S(1)} %get-tuple-element.8.size, f32[8,32,384]{2,1,0:T(8,128)S(1)} %get-tuple-element.9.lm, f32[8,32,384]{2,1,0:T(8,128)S(1)} %get-tuple-element.10.mm, f32[2,384]{1,0:T(2,128)S(1)} %get-tuple-element.11.coef), custom_call_target="tpu_custom_call" | custom-call | tf_op jit(solution)/shard_map/finish/pallas_call | solution.py:402

commit v5 on v4

--- a/solution.py
+++ b/solution.py
@@ -17,7 +17,7 @@
 ROWS = 8
 OFFSET = 8
 AHEAD = 6
-CUTS = (0, 11, 19, 27)
+CUTS = ((30, 2), (0, 11), (11, 8), (19, 8), (27, 3))
 TINY = 1.1754944e-38
 
 
@@ -77,7 +77,8 @@
     members = len(plane_offs) + 1
 
     barrier = pltpu.get_barrier_semaphore()
-    steps = [(1, 0), (-1, 0), (0, 1), (0, -1), (1, 1), (1, -1), (-1, 1), (-1, -1)]
+    beyond = 2 * me[4] - 1
+    steps = [(1, 0), (-1, 0), (0, 1), (0, -1), (1, beyond), (-1, beyond)]
     greeted = [around(*step) for step in steps] + [shifted(in_line, off) for off in line_offs]
     for other in greeted:
         pl.semaphore_signal(barrier, inc=1, device_id=other, device_id_type=MESH)
@@ -115,21 +116,27 @@
         rim(1, (body, first_two), (body, behind), left),
     ]
     strips = []
-    cuts = [(OFFSET + a, b - a) for a, b in zip(CUTS, CUTS[1:] + (depth,))]
+    cuts = [(OFFSET + at, count) for at, count in CUTS]
     for number, cut in enumerate(cuts):
         strips.append((
             rim(2 + 2 * number, ((nx, 2), cut), ((0, 2), cut), up),
             rim(3 + 2 * number, ((2, 2), cut), ((nx + 2, 2), cut), down),
         ))
     first = 2 + 2 * len(cuts)
+    own = jnp.where(outer, last_two[0], first_two[0]), 2
+    far = jnp.where(outer, before[0], behind[0]), 2
+    handed = jnp.where(outer, first_two[0], last_two[0]), 2
+    taken = jnp.where(outer, behind[0], before[0]), 2
     corners = [
-        rim(first, ((nx, 2), last_two), ((0, 2), before), around(1, 1)),
-        rim(first + 1, ((nx, 2), first_two), ((0, 2), behind), around(1, -1)),
-        rim(first + 2, ((2, 2), last_two), ((nx + 2, 2), before), around(-1, 1)),
-        rim(first + 3, ((2, 2), first_two), ((nx + 2, 2), behind), around(-1, -1)),
+        rim(first + 1 - me[4], ((nx, 2), own), ((0, 2), far), around(1, beyond)),
+        rim(first + 3 - me[4], ((2, 2), own), ((nx + 2, 2), far), around(-1, beyond)),
     ]
 
-    for copy in sides + corners + [strip for pair in strips for strip in pair]:
+    def hand(side):
+        rows = (side * (nx + 2), 2)
+        return rim(first + 2 * side + me[4], (rows, handed), (rows, taken), (*me[:4], nc - 1 - me[4]))
+
+    for copy in sides + corners:
         copy.start()
 
     lane = lax.broadcasted_iota(jnp.int32, (ROWS, LANES), 1)
@@ -241,6 +248,14 @@
         edge = jnp.logical_and(k >= models, k != joint)
         spot = jnp.where(second, k - joint - 2, jnp.where(k > joint, tiles, k - models))
 
+        @pl.when(k == 1)
+        def _():
+            for copy in sides:
+                copy.wait_send()
+            for pair in strips:
+                for copy in pair:
+                    copy.start()
+
         @pl.when(k == inner - 1)
         def _():
             sides[0].wait_recv()
@@ -253,12 +268,29 @@
             there = pad.at[:, :, pl.ds(side * (nx + 2), 2), pl.ds(*cut), :]
             pltpu.make_async_copy(there, there, recv_sem.at[number]).wait()
 
-        for number, cut in enumerate(cuts):
-            @pl.when(jnp.logical_and(edge, spot == (number + 1 if number else 0)))
-            def _(number=number, cut=cut):
-                if number == 0:
-                    landed(first + 2 * side, before)
-                landed(2 + 2 * number + side, cut)
+        def strip(number):
+            landed(2 + 2 * number + side, cuts[number])
+
+        @pl.when(jnp.logical_and(edge, spot == 0))
+        def _():
+            strip(0)
+
+            @pl.when(jnp.logical_not(outer))
+            def _():
+                hand(side).start()
+
+            strip(1)
+
+            @pl.when(outer)
+            def _():
+                hand(side).start()
+
+            landed(first + 2 * side, before)
+
+        for number in range(2, len(cuts)):
+            @pl.when(jnp.logical_and(edge, spot == number))
+            def _(number=number):
+                strip(number)
                 if number == len(cuts) - 1:
                     landed(first + 1 + 2 * side, behind)
 
@@ -342,7 +374,7 @@
         coefficient = share / below
         coef_out[0:1, line] = coefficient
         coef_out[1:2, line] = coefficient * gaps[3:4, line]
-    for copy in sides + corners + [strip for pair in strips for strip in pair]:
+    for copy in corners + [hand(0), hand(1)] + [strip for pair in strips for strip in pair]:
         copy.wait_send()
 
 

time: 38.7 us -> 38.3 us (0.990)
  Pallas kernels: 37.9 us -> 37.5 us
    pallas_call x1, Pallas kernels: 36.9 us -> 36.5 us  [per_device(): pl.pallas_call(lambda *refs: kernel(shape, cells, *refs), out_shape=(grid...]
where the time goes in v5:
time: 38.3 us; the launch traced here: 38.1 us
  Pallas kernels  37.5 us (98%)
  between operations  0.64 us (2%)
    pallas_call x1, Pallas kernels, per_device(): pl.pallas_call(lambda *refs: kernel(shape, cells, *refs), out_shape=(grid...  36.5 us
    pallas_call x1, Pallas kernels, per_device(): pl.pallas_call(finish, out_shape=(grid, grid, grid, jax.ShapeDtypeStruct(...  1.05 us

profile of v5, /device:TPU:1, one launch (start us, length us, event | category | flops | bytes accessed | tf_op | source)
XLA Modules:
  0.0 38.1 jit_solution(19690371786920311)
XLA Ops:
  0.6 36.5 %smagorinsky.1 = (f32[8,32,384]{2,1,0:T(8,128)S(1)}, f32[8,32,384]{2,1,0:T(8,128)S(1)}, f32[8,32,384]{2,1,0:T(8,128)S(1)}, f32[2,384]{1,0:T(2,128)S(1)}) custom-call(f32[3,8,32,384]{3,2,1,0:T(8,128)} %refs_0_.1, f32[385]{0:T(512)} %refs_1_.1), custom_call_target="tpu_custom_call" | custom-call | tf_op jit(solution)/shard_map/smagorinsky/pallas_call | solution.py:409
  37.1 1.0 %finish.1 = (f32[8,32,384]{2,1,0:T(8,128)}, f32[8,32,384]{2,1,0:T(8,128)}, f32[8,32,384]{2,1,0:T(8,128)}, f32[384]{0:T(512)}) custom-call(f32[8,32,384]{2,1,0:T(8,128)S(1)} %get-tuple-element.8.size, f32[8,32,384]{2,1,0:T(8,128)S(1)} %get-tuple-element.9.lm, f32[8,32,384]{2,1,0:T(8,128)S(1)} %get-tuple-element.10.mm, f32[2,384]{1,0:T(2,128)S(1)} %get-tuple-element.11.coef), custom_call_target="tpu_custom_call" | custom-call | tf_op jit(solution)/shard_map/finish/pallas_call | solution.py:434

commit v6 on v5

--- a/solution.py
+++ b/solution.py
@@ -71,8 +71,12 @@
         return tuple(spot)
 
     in_plane, in_line = (1, 2, 3), (0, 4)
-    plane_offs = list(itertools.product(range(nxl), range(ny), range(nxh)))[1:]
-    line_offs = [(step, 0) for step in range(1, nz)] + [(step, 1) for step in range(nz)]
+    def hops(off):
+        xl, y, xh = off
+        return min(y, ny - y) + (2 * xh if xl == 0 else 1)
+
+    plane_offs = sorted(list(itertools.product(range(nxl), range(ny), range(nxh)))[1:], key=hops, reverse=True)
+    line_offs = sorted(list(itertools.product(range(nz), range(nc)))[1:], key=lambda off: -min(off[0], nz - off[0]))
     plane_mine = (me[1] * ny + me[2]) * nxh + me[3]
     members = len(plane_offs) + 1
 
@@ -343,10 +347,15 @@
         spot = shifted(in_plane, off)
         return (*spot[:4], nc - 1)
 
+    def left():
+        for copy in corners + [hand(0), hand(1)] + [strip for pair in strips for strip in pair]:
+            copy.wait_send()
+
     @pl.when(jnp.logical_not(outer))
     def _():
-        for off in [(0, 0, 0)] + plane_offs:
+        for off in plane_offs + [(0, 0, 0)]:
             send(0, plane_mine, 1, to_outer(off))
+        left()
         arrived(0, members, sum_send.at[0])
         arrived(line_at, nz, sum_recv.at[2])
 
@@ -355,14 +364,15 @@
         for off in plane_offs:
             send(0, members + plane_mine, 1, shifted(in_plane, off))
         got[members + plane_mine] = sent[0]
+        left()
         arrived(0, 2 * members - 1, sum_recv.at[1])
         whole = added([got[k] for k in range(2 * members)])
         sent[1] = whole
         for off in line_offs:
             send(1, line_at + me[0], 2, shifted(in_line, off))
         got[line_at + me[0]] = whole
+        arrived(0, members - 1, sum_send.at[0])
         arrived(line_at, nz - 1, sum_recv.at[2])
-        arrived(0, members - 1, sum_send.at[0])
         arrived(0, len(line_offs), sum_send.at[0])
 
     total = added([got[line_at + k] for k in range(nz)])
@@ -374,8 +384,6 @@
         coefficient = share / below
         coef_out[0:1, line] = coefficient
         coef_out[1:2, line] = coefficient * gaps[3:4, line]
-    for copy in corners + [hand(0), hand(1)] + [strip for pair in strips for strip in pair]:
-        copy.wait_send()
 
 
 def finish(size, lm, mm, coef, eddy_out, lm_out, mm_out, coef_out, eddy, sem):

time: 38.3 us -> 38.2 us (level)
  no operation moved by 1% of the time
where the time goes in v6:
time: 38.2 us; the launch traced here: 38.1 us
  Pallas kernels  37.5 us (98%)
  between operations  0.64 us (2%)
    pallas_call x1, Pallas kernels, per_device(): pl.pallas_call(lambda *refs: kernel(shape, cells, *refs), out_shape=(grid...  36.4 us
    pallas_call x1, Pallas kernels, per_device(): pl.pallas_call(finish, out_shape=(grid, grid, grid, jax.ShapeDtypeStruct(...  1.05 us

profile of v6, /device:TPU:1, one launch (start us, length us, event | category | flops | bytes accessed | tf_op | source)
XLA Modules:
  0.0 38.1 jit_solution(17337648237414871794)
XLA Ops:
  0.6 36.4 %smagorinsky.1 = (f32[8,32,384]{2,1,0:T(8,128)S(1)}, f32[8,32,384]{2,1,0:T(8,128)S(1)}, f32[8,32,384]{2,1,0:T(8,128)S(1)}, f32[2,384]{1,0:T(2,128)S(1)}) custom-call(f32[3,8,32,384]{3,2,1,0:T(8,128)} %refs_0_.1, f32[385]{0:T(512)} %refs_1_.1), custom_call_target="tpu_custom_call" | custom-call | tf_op jit(solution)/shard_map/smagorinsky/pallas_call | solution.py:417
  37.1 1.0 %finish.1 = (f32[8,32,384]{2,1,0:T(8,128)}, f32[8,32,384]{2,1,0:T(8,128)}, f32[8,32,384]{2,1,0:T(8,128)}, f32[384]{0:T(512)}) custom-call(f32[8,32,384]{2,1,0:T(8,128)S(1)} %get-tuple-element.8.size, f32[8,32,384]{2,1,0:T(8,128)S(1)} %get-tuple-element.9.lm, f32[8,32,384]{2,1,0:T(8,128)S(1)} %get-tuple-element.10.mm, f32[2,384]{1,0:T(2,128)S(1)} %get-tuple-element.11.coef), custom_call_target="tpu_custom_call" | custom-call | tf_op jit(solution)/shard_map/finish/pallas_call | solution.py:442
